TPU v7x, 512 devices: a whole 4x8x8 slice. The times are simulated.
512 devices in a mesh: tile: 128 (over z_hi, x, y, core), lev: 4 (over z_lo).
Axes of the slice: x: 4, y: 8, z: 8 (z_hi: 2, z_lo: 4; z = z_hi * 4 + z_lo), core: 2. Of those that a mesh axis runs over, the one named last changes fastest.
Arguments:
- members_pert: bfloat16 [64, 16, 524288], P('lev', None, 'tile'), may hold values from -4 to 4
- coarse_pert: bfloat16 [64, 8, 32768], P('lev', None, 'tile'), may hold values from -6 to 6
- member_ctrl: bfloat16 [64, 16, 32768], P('lev', None, 'tile'), may hold values from -6 to 6
- coarse_ctrl: bfloat16 [64, 8, 32768], P('lev', None, 'tile'), may hold values from -6 to 6
- vert_loc: float32 [64, 64], replicated, may hold values from -1.5 to 1.5, as said below
- stencil: int32 [4, 524288], P(None, 'tile'), may hold values from 0 to 383, as said below
- interp_w: bfloat16 [4, 524288], P(None, 'tile'), may hold values from 0 to 1, as said below
Outputs:
- member_out: float32 [64, 16, 32768], P('lev', None, 'tile')
- coarse_out: float32 [64, 8, 32768], P('lev', None, 'tile')
Inputs may be any that keep to these rules, and one draw needn't show every extreme that they name: vert_loc[i, j] is zero where |i - j| > 4, and nonzero where |i - j| = 4. stencil indexes a window of 384 coarse cells of the fine cell's tile index: the last 64 coarse cells of the tile index before it (the first one's predecessor is the last), its own 256 cells, then the first 64 cells of the tile index after it; the four corners of a fine cell are distinct. `interp_w`: the four weights of a fine cell are nonnegative and sum to one up to rounding.
All inputs are finite; a program needn't handle non-finite values.
Results may differ from a plain program's by a relative error of at most 0.013.
Values may be sent and summed in bfloat16 or wider, within the bound.
No kernel may reach another device: no remote copies, remote signals or barrier semaphores. Data moves between devices by JAX's collectives and lax.ppermute only.
A program may use at most 64 MiB of HBM per device.

v0:
```python
import jax
import jax.numpy as jnp
from jax import lax
from jax.sharding import PartitionSpec as P

HB = 4
CW = 64


def extended(value, sides, width, wrap):
    for axis, dim in sides:
        size, length = (lax.axis_size(axis), value.shape[dim])
        up = [(i, (i + 1) % size) for i in range(size if wrap else size - 1)]
        down = [(j, i) for i, j in up]
        last = lax.slice_in_dim(value, length - width, length, axis=dim)
        leading = lax.slice_in_dim(value, 0, width, axis=dim)
        before = lax.ppermute(last, axis, up)
        after = lax.ppermute(leading, axis, down)
        value = jnp.concatenate([before, value, after], axis=dim)
    return value


def shifted(value, axis, by):
    size = lax.axis_size(axis)
    return lax.ppermute(value, axis, [(i, (i + by) % size) for i in range(size)])


def from_behind(value, axis, by):
    size = lax.axis_size(axis)
    pairs = [(i, i + by) for i in range(size) if 0 <= i + by < size]
    return lax.ppermute(value, axis, pairs)


def shards(members_pert, coarse_pert, member_ctrl, coarse_ctrl, vert_loc, stencil, interp_w):
    highest = lax.Precision.HIGHEST
    level_rows = member_ctrl.shape[0]
    members = member_ctrl.shape[1]
    coarse_cells = member_ctrl.shape[2]
    fine_cells = members_pert.shape[2]
    kinds = members + 1
    stacked = jnp.concatenate([member_ctrl, coarse_ctrl], axis=1)
    widened = extended(stacked, (("lev", 0),), HB, False)
    first_level = lax.axis_index("lev") * level_rows
    padded = jnp.pad(vert_loc, ((0, 0), (HB, HB)))
    band_rows = lax.dynamic_slice(
        padded, (first_level, first_level), (level_rows, level_rows + 2 * HB)
    )
    localized = jnp.einsum("ij,jkc->ikc", band_rows, widened.astype(jnp.float32), precision=highest)
    loc_members = localized[:, :members].astype(jnp.bfloat16)
    loc_coarse = localized[:, members:].astype(jnp.bfloat16)
    combined = jnp.sum(
        coarse_pert.astype(jnp.float32) * loc_coarse.astype(jnp.float32), axis=1
    ).astype(jnp.bfloat16)
    fields = jnp.concatenate([loc_members, combined[:, None, :]], axis=1)
    window = extended(fields, (("tile", 2),), CW, True)
    window_span = window.shape[2]
    cell_rows = lax.broadcasted_iota(jnp.int32, (window_span, fine_cells), 0)
    nothing = jnp.zeros((), jnp.bfloat16)
    interp_matrix = jnp.zeros((window_span, fine_cells), jnp.bfloat16)
    for corner in range(4):
        interp_matrix = interp_matrix + jnp.where(
            cell_rows == stencil[corner][None, :], interp_w[corner][None, :], nothing
        )
    flattened = window.reshape(level_rows * kinds, window_span)
    interp = jnp.dot(flattened, interp_matrix, preferred_element_type=jnp.float32).reshape(
        level_rows, kinds, fine_cells
    )
    pert_float = members_pert.astype(jnp.float32)
    increment = jnp.sum(pert_float * interp[:, :members], axis=1) + interp[:, members]
    adjoint = jnp.concatenate(
        [pert_float * increment[:, None, :], increment[:, None, :]], axis=1
    ).astype(jnp.bfloat16)
    coarse_adjoint = lax.dot_general(
        adjoint.reshape(level_rows * kinds, fine_cells),
        interp_matrix,
        (((1,), (1,)), ((), ())),
        preferred_element_type=jnp.float32,
    )
    coarse_adjoint = coarse_adjoint.reshape(level_rows, kinds, window_span)
    own_cells = coarse_adjoint[:, :, CW : CW + coarse_cells]
    from_next = shifted(coarse_adjoint[:, :, :CW].astype(jnp.bfloat16), "tile", -1).astype(
        jnp.float32
    )
    from_prev = shifted(
        coarse_adjoint[:, :, CW + coarse_cells :].astype(jnp.bfloat16), "tile", 1
    ).astype(jnp.float32)
    gathered = (
        own_cells
        + jnp.pad(from_next, ((0, 0), (0, 0), (coarse_cells - CW, 0)))
        + jnp.pad(from_prev, ((0, 0), (0, 0), (0, coarse_cells - CW)))
    )
    adjoint_ctrl = jnp.concatenate(
        [
            gathered[:, :members],
            coarse_pert.astype(jnp.float32) * gathered[:, members : members + 1],
        ],
        axis=1,
    )
    spread = jnp.einsum("ij,ikc->jkc", band_rows, adjoint_ctrl, precision=highest)
    from_above = from_behind(spread[:HB].astype(jnp.bfloat16), "lev", -1).astype(jnp.float32)
    from_below = from_behind(spread[level_rows + HB :].astype(jnp.bfloat16), "lev", 1).astype(
        jnp.float32
    )
    result = spread[HB : HB + level_rows]
    result = result + jnp.pad(from_below, ((0, level_rows - HB), (0, 0), (0, 0)))
    result = result + jnp.pad(from_above, ((level_rows - HB, 0), (0, 0), (0, 0)))
    return (result[:, :members], result[:, members:])


def solution(mesh):
    in_specs = (
        P("lev", None, "tile"),
        P("lev", None, "tile"),
        P("lev", None, "tile"),
        P("lev", None, "tile"),
        P(),
        P(None, "tile"),
        P(None, "tile"),
    )
    out_specs = (P("lev", None, "tile"), P("lev", None, "tile"))
    return jax.shard_map(shards, mesh=mesh, in_specs=in_specs, out_specs=out_specs, check_vma=False)
```

profile of v0, /device:TPU:64, one launch (start us, length us, event | category | flops | bytes accessed | tf_op | source)
XLA Modules:
  0.0 80.5 jit_solution(5642765467144369191)
XLA Ops:
  0.6 0.9 %copy_dynamic-update-slice_fusion = bf16[16,24,256]{2,0,1:T(8,128)(2,1)S(1)} fusion(bf16[16,16,256]{2,1,0:T(8,128)(2,1)} %param.9), kind=kLoop, calls=%fused_computation.43 | loop fusion | bytes 262144
  1.6 0.9 %copy_dynamic-update-slice_fusion.1 = bf16[16,24,256]{2,0,1:T(8,128)(2,1)S(1)} fusion(bf16[16,24,256]{2,0,1:T(8,128)(2,1)S(1)} %copy_dynamic-update-slice_fusion, bf16[16,8,256]{2,1,0:T(8,128)(2,1)} %param.10), kind=kLoop, calls=%fused_computation.46 | loop fusion | bytes 131072 | tf_op jit(solution)/shard_map/concatenate | solution.py:41
  2.5 4.3 %collective-permute-start = (bf16[4,24,256]{2,0,1:T(4,128)(2,1)S(1)}, bf16[4,24,256]{2,0,1:T(4,128)(2,1)S(1)}, u32[]{:S(2)}, u32[]{:S(2)}) collective-permute-start(bf16[4,24,256]{2,0,1:T(4,128)(2,1)S(1)} %get-tuple-element.14), channel_id=1, source_target_pairs={{0,1},{1,2},{2,3},{4,5},{5,6},{6,7},{8,9},{9,10},{10,11},{12,13},{... | collective-permute-start | bytes 147464 | tf_op jit(solution)/shard_map/ppermute | solution.py:17
  6.8 3.9 %collective-permute-start.1 = (bf16[4,24,256]{2,0,1:T(4,128)(2,1)S(1)}, bf16[4,24,256]{2,0,1:T(4,128)(2,1)S(1)}, u32[]{:S(2)}, u32[]{:S(2)}) collective-permute-start(bf16[4,24,256]{2,0,1:T(4,128)(2,1)S(1)} %get-tuple-element.15), channel_id=1, source_target_pairs={{1,0},{2,1},{3,2},{5,4},{6,5},{7,6},{9,8},{10,9},{11,10},{13,12},{... | collective-permute-start | bytes 147464 | tf_op jit(solution)/shard_map/ppermute | solution.py:18
  10.7 1.1 %fusion.42 = (s32[1,4096]{1,0:T(1,128)S(1)}, s32[1,4096]{1,0:T(1,128)S(1)}, s32[1,4096]{1,0:T(1,128)S(1)}, s32[1,4096]{1,0:T(1,128)S(1)}) fusion(s32[4,4096]{1,0:T(4,128)} %param.12), kind=kLoop, calls=%fused_computation.65 | loop fusion | bytes 131072 | tf_op jit(solution)/shard_map/slice | solution.py:62
  11.8 1.3 %collective-permute-done.1 = bf16[4,24,256]{2,0,1:T(4,128)(2,1)S(1)} collective-permute-done((bf16[4,24,256]{2,0,1:T(4,128)(2,1)S(1)}, bf16[4,24,256]{2,0,1:T(4,128)(2,1)S(1)}, u32[]{:S(2)}, u32[]{:S(2)}) %collective-permute-start.1) | collective-permute-done | bytes 49184 | tf_op jit(solution)/shard_map/ppermute | solution.py:18
  13.1 1.1 %convolution_convert_fusion = bf16[16,24,256]{2,0,1:T(8,128)(2,1)S(1)} fusion(bf16[4,24,256]{2,0,1:T(4,128)(2,1)S(1)} %collective-permute-done.1, bf16[16,24,256]{2,0,1:T(8,128)(2,1)S(1)} %copy_dynamic-update-slice_fusion.1, bf16[4,24,256]{2,0,1:T(4,128)(2,1)S(1)} %collective-permute-done, s32[]{:T(128)S(6)} %select_n.19, s32[]{:T(128)S(6)} %select_n.20, ...), kind=kOutput, calls=%fused_computation.21 | convolution fusion | flops 29294592 | bytes 507912 | tf_op jit(solution)/shard_map/ij,jkc->ikc/dot_general | solution.py:48
  14.2 0.9 %fusion.27 = bf16[16,256]{1,0:T(8,128)(2,1)S(1)} fusion(bf16[16,24,256]{2,0,1:T(8,128)(2,1)S(1)} %convolution_convert_fusion, bf16[16,8,256]{2,1,0:T(8,128)(2,1)} %param.8), kind=kLoop, calls=%fused_computation.42 | loop fusion | flops 126976 | bytes 139264 | tf_op jit(solution)/shard_map/reduce_sum | solution.py:51
  15.2 1.9 %collective-permute-start.2 = (bf16[16,17,64]{2,0,1:T(8,128)(2,1)S(1)}, bf16[16,17,64]{2,0,1:T(8,128)(2,1)S(1)}, u32[]{:S(2)}, u32[]{:S(2)}) collective-permute-start(bf16[16,17,64]{2,0,1:T(8,128)(2,1)S(1)} %get-tuple-element.16), channel_id=1, source_target_pairs={{0,4},{4,8},{8,12},{12,16},{16,20},{20,24},{24,28},{28,32},{32,36}... | collective-permute-start | bytes 104456 | tf_op jit(solution)/shard_map/ppermute | solution.py:17
  17.1 11.9 %collective-permute-start.3 = (bf16[16,17,64]{2,0,1:T(8,128)(2,1)S(1)}, bf16[16,17,64]{2,0,1:T(8,128)(2,1)S(1)}, u32[]{:S(2)}, u32[]{:S(2)}) collective-permute-start(bf16[16,17,64]{2,0,1:T(8,128)(2,1)S(1)} %get-tuple-element.17), channel_id=1, source_target_pairs={{4,0},{8,4},{12,8},{16,12},{20,16},{24,20},{28,24},{32,28},{36,32}... | collective-permute-start | bytes 104456 | tf_op jit(solution)/shard_map/ppermute | solution.py:18
  29.0 1.1 %slice_reduce_fusion.3 = (bf16[4096]{0:T(1024)(128)(2,1)S(1)}, bf16[4096]{0:T(1024)(128)(2,1)S(1)}, bf16[4096]{0:T(1024)(128)(2,1)S(1)}, bf16[4096]{0:T(1024)(128)(2,1)S(1)}) fusion(bf16[4,4096]{1,0:T(4,128)(2,1)} %param.13), kind=kLoop, calls=%fused_computation.52 | loop fusion | bytes 65536 | tf_op jit(solution)/shard_map/slice | solution.py:62
  30.1 0.8 %collective-permute-done.3 = bf16[16,17,64]{2,0,1:T(8,128)(2,1)S(1)} collective-permute-done((bf16[16,17,64]{2,0,1:T(8,128)(2,1)S(1)}, bf16[16,17,64]{2,0,1:T(8,128)(2,1)S(1)}, u32[]{:S(2)}, u32[]{:S(2)}) %collective-permute-start.3) | collective-permute-done | bytes 34848 | tf_op jit(solution)/shard_map/ppermute | solution.py:18
  30.9 0.1 pad_maximum_fusion.1
  31.1 3.6 %fusion.15 = f32[16,17,4096]{2,1,0:T(8,128)S(1)} fusion(s32[4096]{0:T(1024)S(1)} %bitcast.33, s32[4096]{0:T(1024)S(1)} %bitcast.35, s32[4096]{0:T(1024)S(1)} %bitcast.31, s32[4096]{0:T(1024)S(1)} %bitcast.29, bf16[4096]{0:T(1024)(128)(2,1)S(1)} %get-tuple-element.6, bf16[4096]{0:T(1024)(128)(2,1)S(1)} %get-tuple-element.7, ...), kind=kOutput, calls=%fused_computation.20 | convolution fusion | flops 880803840 | bytes 4763648 | tf_op jit(solution)/shard_map/dot_general | solution.py:65
  34.7 1.0 %fusion.4 = f32[16,4096]{1,0:T(8,128)S(1)} fusion(bf16[16,16,4096]{2,1,0:T(8,128)(2,1)S(1)} %copy-done, f32[16,17,4096]{2,1,0:T(8,128)S(1)} %fusion.15), kind=kLoop, calls=%fused_computation.10 | loop fusion | flops 3080192 | bytes 6553600 | tf_op jit(solution)/shard_map/reduce_sum | solution.py:69
  35.7 0.5 fusion.38
  36.2 0.2 copy.31
  36.4 0.5 fusion.5
  36.9 4.1 %fusion.43 = (bf16[16,17,384]{2,1,0:T(8,128)(2,1)S(1)}, f32[16,17,384]{2,1,0:T(8,128)S(1)}) fusion(s32[4096]{0:T(1024)S(1)} %bitcast.34, s32[4096]{0:T(1024)S(1)} %bitcast.36, s32[4096]{0:T(1024)S(1)} %bitcast.32, s32[4096]{0:T(1024)S(1)} %bitcast.30, bf16[4096]{0:T(1024)(128)(2,1)S(1)} %get-tuple-element.6, bf16[4096]{0:T(1024)(128)(2,1)S(1)} %get-tuple-element.7, ...), kind=kOutput, calls=%fused_computation.66 | convolution fusion | flops 885364736 | bytes 2953216 | tf_op jit(solution)/shard_map/dot_general | solution.py:73
  41.0 0.1 fusion.40
  41.1 12.1 %collective-permute-start.4 = (bf16[16,17,64]{2,1,0:T(8,128)(2,1)S(1)}, bf16[16,17,64]{2,1,0:T(8,128)(2,1)S(1)}, u32[]{:S(2)}, u32[]{:S(2)}) collective-permute-start(bf16[16,17,64]{2,1,0:T(8,128)(2,1)S(1)} %get-tuple-element.12), channel_id=1, source_target_pairs={{0,508},{4,0},{8,4},{12,8},{16,12},{20,16},{24,20},{28,24},{32,28}... | collective-permute-start | bytes 104456 | tf_op jit(solution)/shard_map/ppermute | solution.py:25
  53.2 1.9 %collective-permute-start.5 = (bf16[16,17,64]{2,1,0:T(8,128)(2,1)S(1)}, bf16[16,17,64]{2,1,0:T(8,128)(2,1)S(1)}, u32[]{:S(2)}, u32[]{:S(2)}) collective-permute-start(bf16[16,17,64]{2,1,0:T(8,128)(2,1)S(1)} %get-tuple-element.13), channel_id=1, source_target_pairs={{0,4},{4,8},{8,12},{12,16},{16,20},{20,24},{24,28},{28,32},{32,36}... | collective-permute-start | bytes 104456 | tf_op jit(solution)/shard_map/ppermute | solution.py:25
  55.2 0.3 collective-permute-done.4
  55.4 12.5 %collective-permute-done.5 = bf16[16,17,64]{2,1,0:T(8,128)(2,1)S(1)} collective-permute-done((bf16[16,17,64]{2,1,0:T(8,128)(2,1)S(1)}, bf16[16,17,64]{2,1,0:T(8,128)(2,1)S(1)}, u32[]{:S(2)}, u32[]{:S(2)}) %collective-permute-start.5) | collective-permute-done | bytes 34848 | tf_op jit(solution)/shard_map/ppermute | solution.py:25
  68.0 0.2 fusion.18
  68.4 0.8 fusion.44
  69.2 3.6 %collective-permute-start.6 = (bf16[4,24,256]{2,0,1:T(4,128)(2,1)S(1)}, bf16[4,24,256]{2,0,1:T(4,128)(2,1)S(1)}, u32[]{:S(2)}, u32[]{:S(2)}) collective-permute-start(bf16[4,24,256]{2,0,1:T(4,128)(2,1)S(1)} %get-tuple-element.10), channel_id=1, source_target_pairs={{0,1},{1,2},{2,3},{4,5},{5,6},{6,7},{8,9},{9,10},{10,11},{12,13},{... | collective-permute-start | bytes 147464 | tf_op jit(solution)/shard_map/ppermute | solution.py:31
  72.8 2.2 %collective-permute-start.7 = (bf16[4,24,256]{2,0,1:T(4,128)(2,1)S(1)}, bf16[4,24,256]{2,0,1:T(4,128)(2,1)S(1)}, u32[]{:S(2)}, u32[]{:S(2)}) collective-permute-start(bf16[4,24,256]{2,0,1:T(4,128)(2,1)S(1)} %get-tuple-element.11), channel_id=1, source_target_pairs={{1,0},{2,1},{3,2},{5,4},{6,5},{7,6},{9,8},{10,9},{11,10},{13,12},{... | collective-permute-start | bytes 147464 | tf_op jit(solution)/shard_map/ppermute | solution.py:31
  75.1 0.1 collective-permute-done.6
  75.2 3.6 %collective-permute-done.7 = bf16[4,24,256]{2,0,1:T(4,128)(2,1)S(1)} collective-permute-done((bf16[4,24,256]{2,0,1:T(4,128)(2,1)S(1)}, bf16[4,24,256]{2,0,1:T(4,128)(2,1)S(1)}, u32[]{:S(2)}, u32[]{:S(2)}) %collective-permute-start.7) | collective-permute-done | bytes 49184 | tf_op jit(solution)/shard_map/ppermute | solution.py:31
  78.9 0.9 %copy.15 = f32[16,16,256]{2,1,0:T(8,128)} copy(f32[16,16,256]{2,0,1:T(8,128)S(1)} %slice.126) | data formatting | bytes 524288
  79.8 0.7 copy.16
  (21 shorter events, 0.5 us)
Async XLA Ops:
  2.5 9.3 %collective-permute-start = (bf16[4,24,256]{2,0,1:T(4,128)(2,1)S(1)}, bf16[4,24,256]{2,0,1:T(4,128)(2,1)S(1)}, u32[]{:S(2)}, u32[]{:S(2)}) collective-permute-start(bf16[4,24,256]{2,0,1:T(4,128)(2,1)S(1)} %get-tuple-element.14), channel_id=1, source_target_pairs={{0,1},{1,2},{2,3},{4,5},{5,6},{6,7},{8,9},{9,10},{10,11},{12,13},{... | collective-permute-start | bytes 147464 | tf_op jit(solution)/shard_map/ppermute | solution.py:17
  6.8 6.3 %collective-permute-start.1 = (bf16[4,24,256]{2,0,1:T(4,128)(2,1)S(1)}, bf16[4,24,256]{2,0,1:T(4,128)(2,1)S(1)}, u32[]{:S(2)}, u32[]{:S(2)}) collective-permute-start(bf16[4,24,256]{2,0,1:T(4,128)(2,1)S(1)} %get-tuple-element.15), channel_id=1, source_target_pairs={{1,0},{2,1},{3,2},{5,4},{6,5},{7,6},{9,8},{10,9},{11,10},{13,12},{... | collective-permute-start | bytes 147464 | tf_op jit(solution)/shard_map/ppermute | solution.py:18
  15.2 14.9 %collective-permute-start.2 = (bf16[16,17,64]{2,0,1:T(8,128)(2,1)S(1)}, bf16[16,17,64]{2,0,1:T(8,128)(2,1)S(1)}, u32[]{:S(2)}, u32[]{:S(2)}) collective-permute-start(bf16[16,17,64]{2,0,1:T(8,128)(2,1)S(1)} %get-tuple-element.16), channel_id=1, source_target_pairs={{0,4},{4,8},{8,12},{12,16},{16,20},{20,24},{24,28},{28,32},{32,36}... | collective-permute-start | bytes 104456 | tf_op jit(solution)/shard_map/ppermute | solution.py:17
  17.1 13.8 %collective-permute-start.3 = (bf16[16,17,64]{2,0,1:T(8,128)(2,1)S(1)}, bf16[16,17,64]{2,0,1:T(8,128)(2,1)S(1)}, u32[]{:S(2)}, u32[]{:S(2)}) collective-permute-start(bf16[16,17,64]{2,0,1:T(8,128)(2,1)S(1)} %get-tuple-element.17), channel_id=1, source_target_pairs={{4,0},{8,4},{12,8},{16,12},{20,16},{24,20},{28,24},{32,28},{36,32}... | collective-permute-start | bytes 104456 | tf_op jit(solution)/shard_map/ppermute | solution.py:18
  31.1 3.6 %copy-start = (bf16[16,16,4096]{2,1,0:T(8,128)(2,1)S(1)}, bf16[16,16,4096]{2,1,0:T(8,128)(2,1)}, u32[]{:S(2)}) copy-start(bf16[16,16,4096]{2,1,0:T(8,128)(2,1)} %param.7) | copy-start | bytes 6291460
  36.9 31.3 %copy-start.1 = (bf16[16,8,256]{2,1,0:T(8,128)(2,1)S(1)}, bf16[16,8,256]{2,1,0:T(8,128)(2,1)}, u32[]{:S(2)}) copy-start(bf16[16,8,256]{2,1,0:T(8,128)(2,1)} %param.8) | copy-start | bytes 196612
  36.9 31.5 %copy-start.2 = (f32[64,64]{1,0:T(8,128)S(1)}, f32[64,64]{1,0:T(8,128)}, u32[]{:S(2)}) copy-start(f32[64,64]{1,0:T(8,128)} %param.11) | copy-start | bytes 49156
  41.1 14.3 %collective-permute-start.4 = (bf16[16,17,64]{2,1,0:T(8,128)(2,1)S(1)}, bf16[16,17,64]{2,1,0:T(8,128)(2,1)S(1)}, u32[]{:S(2)}, u32[]{:S(2)}) collective-permute-start(bf16[16,17,64]{2,1,0:T(8,128)(2,1)S(1)} %get-tuple-element.12), channel_id=1, source_target_pairs={{0,508},{4,0},{8,4},{12,8},{16,12},{20,16},{24,20},{28,24},{32,28}... | collective-permute-start | bytes 104456 | tf_op jit(solution)/shard_map/ppermute | solution.py:25
  53.2 14.7 %collective-permute-start.5 = (bf16[16,17,64]{2,1,0:T(8,128)(2,1)S(1)}, bf16[16,17,64]{2,1,0:T(8,128)(2,1)S(1)}, u32[]{:S(2)}, u32[]{:S(2)}) collective-permute-start(bf16[16,17,64]{2,1,0:T(8,128)(2,1)S(1)} %get-tuple-element.13), channel_id=1, source_target_pairs={{0,4},{4,8},{8,12},{12,16},{16,20},{20,24},{24,28},{28,32},{32,36}... | collective-permute-start | bytes 104456 | tf_op jit(solution)/shard_map/ppermute | solution.py:25
  69.2 6.0 %collective-permute-start.6 = (bf16[4,24,256]{2,0,1:T(4,128)(2,1)S(1)}, bf16[4,24,256]{2,0,1:T(4,128)(2,1)S(1)}, u32[]{:S(2)}, u32[]{:S(2)}) collective-permute-start(bf16[4,24,256]{2,0,1:T(4,128)(2,1)S(1)} %get-tuple-element.10), channel_id=1, source_target_pairs={{0,1},{1,2},{2,3},{4,5},{5,6},{6,7},{8,9},{9,10},{10,11},{12,13},{... | collective-permute-start | bytes 147464 | tf_op jit(solution)/shard_map/ppermute | solution.py:31
  72.8 6.0 %collective-permute-start.7 = (bf16[4,24,256]{2,0,1:T(4,128)(2,1)S(1)}, bf16[4,24,256]{2,0,1:T(4,128)(2,1)S(1)}, u32[]{:S(2)}, u32[]{:S(2)}) collective-permute-start(bf16[4,24,256]{2,0,1:T(4,128)(2,1)S(1)} %get-tuple-element.11), channel_id=1, source_target_pairs={{1,0},{2,1},{3,2},{5,4},{6,5},{7,6},{9,8},{10,9},{11,10},{13,12},{... | collective-permute-start | bytes 147464 | tf_op jit(solution)/shard_map/ppermute | solution.py:31
where the time goes:
time: 81.1 us; the launch traced here: 80.5 us
  starting transfers between devices  41.8 us (52%)
  waiting for transfers between devices  18.7 us (23%)
  matrix products  9.56 us (12%)
  local copies, waits for them, and re-layouts  6.07 us (7%)
  other arithmetic  3.43 us (4%)
  between operations  0.93 us (1%)
    ppermute x2, starting transfers between devices, extended(): after = lax.ppermute(leading, axis, down)  15.8 us
    ppermute x2, starting transfers between devices, shifted(): lax.ppermute(value, axis, [(i, (i + by) % size) for i in range(size)])  14 us
    ppermute x2, waiting for transfers between devices, shifted(): lax.ppermute(value, axis, [(i, (i + by) % size) for i in range(size)])  12.8 us
    ppermute x2, starting transfers between devices, extended(): before = lax.ppermute(last, axis, up)  6.2 us
    ppermute x2, starting transfers between devices, from_behind(): return lax.ppermute(value, axis, pairs)  5.84 us
    dot_general x1, matrix products, shards(): lax.dot_general(adjoint.reshape(level_rows * kinds, fine_cells), interp_m...  4.14 us
    ppermute x2, waiting for transfers between devices, from_behind(): return lax.ppermute(value, axis, pairs)  3.75 us
    dot_general x1, matrix products, shards(): jnp.dot(flattened, interp_matrix, preferred_element_type=jnp.float32)  3.56 us
  transfers between devices with their start and end apart: 8, of which 6 were waited for; matrix products, arithmetic and copies ran while one was open for 3% of the time, Pallas kernels for 0%

commit v1 on v0

v1 whole, which is shorter than its diff:
```python
import jax
import jax.numpy as jnp
from jax import lax
from jax.experimental import pallas as pl
from jax.experimental.pallas import tpu as pltpu
from jax.sharding import PartitionSpec as P


HB = 4
CW = 64
LV = 16
MB = 16
CM = 8
ND = 256
NF = 4096
WL = LV + 2 * HB
ROWS = LV * MB + LV
HALF = 144
SPAN = ND + 2 * CW
BLOCK = 512
F32 = jnp.float32
BF16 = jnp.bfloat16
SMEM = pl.BlockSpec(memory_space=pltpu.SMEM)
VMEM = pl.BlockSpec(memory_space=pltpu.VMEM)


def low_lanes(shape):
    return lax.broadcasted_iota(jnp.int32, shape, 1) < CW


def turn(value):
    return pltpu.roll(value, CW, 1)


def gather_kernel(mc_hbm, cc_hbm, cp_hbm, stencil_hbm, weight_hbm, top, bottom, mc, cc, cp, stencil, weight, sems):
    moves = [
        (mc_hbm.at[pl.ds(LV - HB, HB)], top.at[:, pl.ds(0, MB)]),
        (cc_hbm.at[pl.ds(LV - HB, HB)], top.at[:, pl.ds(MB, CM)]),
        (mc_hbm.at[pl.ds(0, HB)], bottom.at[:, pl.ds(0, MB)]),
        (cc_hbm.at[pl.ds(0, HB)], bottom.at[:, pl.ds(MB, CM)]),
        (mc_hbm, mc),
        (cc_hbm, cc),
        (cp_hbm, cp),
        (stencil_hbm, stencil),
        (weight_hbm, weight),
    ]
    copies = [pltpu.make_async_copy(source, target, sems.at[k]) for k, (source, target) in enumerate(moves)]
    for copy in copies:
        copy.start()
    for copy in copies:
        copy.wait()


def localize_kernel(odd_ref, band_ref, mc_ref, cc_ref, below_ref, above_ref, cp_ref, own_ref, chip_ref, cross_ref, ms, cs, full):
    for j in range(WL):
        if j < HB:
            ms[j] = below_ref[j, :MB].astype(F32)
            cs[j] = below_ref[j, MB:].astype(F32)
        elif j < HB + LV:
            ms[j] = mc_ref[j - HB].astype(F32)
            cs[j] = cc_ref[j - HB].astype(F32)
        else:
            ms[j] = above_ref[j - HB - LV, :MB].astype(F32)
            cs[j] = above_ref[j - HB - LV, MB:].astype(F32)
    full[ROWS:] = jnp.zeros((2 * HALF - ROWS, ND), F32)
    for i in range(LV):
        member = band_ref[i, i] * ms[i]
        coarse = band_ref[i, i] * cs[i]
        for j in range(i + 1, i + 2 * HB + 1):
            member = member + band_ref[i, j] * ms[j]
            coarse = coarse + band_ref[i, j] * cs[j]
        full[i * MB : (i + 1) * MB] = member
        coarse = coarse.astype(BF16).astype(F32)
        full[LV * MB + i : LV * MB + i + 1] = jnp.sum(cp_ref[i].astype(F32) * coarse, axis=0, keepdims=True)
    own_ref[...] = full[:ROWS].astype(BF16)
    odd = odd_ref[0] == 1
    first = full[:, : 2 * CW]
    last = full[:, ND - 2 * CW :]
    low = low_lanes((HALF, 2 * CW))
    first = jnp.where(low, first[:HALF], turn(first[HALF:]))
    last = jnp.where(low, turn(last[:HALF]), last[HALF:])
    cross_ref[...] = jnp.where(odd, last, first).astype(BF16)
    chip_ref[...] = jnp.where(odd, first, last).astype(BF16)


def weights_kernel(odd_ref, stencil_ref, weight_ref, pert_hbm, out_ref, pert_ref, sem):
    fetch = pltpu.make_async_copy(pert_hbm, pert_ref, sem)
    fetch.start()
    odd = odd_ref[0]
    rows = 16
    for start in range(0, NF, BLOCK):
        span = pl.ds(start, BLOCK)
        row = lax.broadcasted_iota(jnp.int32, (rows, BLOCK), 0)
        cells = [jnp.broadcast_to(stencil_ref[q : q + 1, span], (rows, BLOCK)) - row for q in range(4)]
        weights = [jnp.broadcast_to(weight_ref[q : q + 1, span].astype(F32), (rows, BLOCK)) for q in range(4)]
        for base in range(0, SPAN, rows):
            if base < ND:
                cell = base + CW
            elif base < ND + CW:
                cell = base - ND + (1 - odd) * (ND + CW)
            else:
                cell = base - ND - CW + odd * (ND + CW)
            value = jnp.where(cells[0] == cell, weights[0], 0.0)
            for q in range(1, 4):
                value = jnp.where(cells[q] == cell, weights[q], value)
            out_ref[base : base + rows, span] = value.astype(BF16)
    fetch.wait()


def fine_kernel(own_ref, chip_ref, cross_ref, matrix_ref, pert, own_out, chip_out, cross_out, field):
    chip = chip_ref[...].astype(F32)
    cross = cross_ref[...].astype(F32)
    low = low_lanes((HALF, 2 * CW))
    field[:, :ND] = own_ref[...]
    field[:HALF, ND:] = jnp.where(low, chip, turn(cross)).astype(BF16)
    field[HALF:, ND:] = jnp.where(low, turn(chip), cross)[: ROWS - HALF].astype(BF16)
    total = jnp.zeros((ROWS, SPAN), F32)
    for b in range(NF // BLOCK):
        span = pl.ds(b * BLOCK, BLOCK)
        matrix = matrix_ref[:, span]
        interp = jnp.dot(field[...], matrix, preferred_element_type=F32)
        member = pert[:, span].astype(F32).reshape(LV, MB, BLOCK)
        increment = jnp.sum(member * interp[: LV * MB].reshape(LV, MB, BLOCK), axis=1) + interp[LV * MB :]
        adjoint = (member * increment[:, None, :]).astype(BF16).reshape(LV * MB, BLOCK)
        adjoint = jnp.concatenate([adjoint, increment.astype(BF16)], axis=0)
        total = total + lax.dot_general(adjoint, matrix, (((1,), (1,)), ((), ())), preferred_element_type=F32)
    own_out[...] = total[:, :ND]
    top = total[:HALF, ND:]
    bottom = jnp.concatenate([total[HALF:, ND:], jnp.zeros((2 * HALF - ROWS, 2 * CW), F32)], axis=0)
    chip_out[...] = jnp.where(low, top, turn(bottom)).astype(BF16)
    cross_out[...] = jnp.where(low, turn(top), bottom).astype(BF16)


def spread_kernel(odd_ref, band_ref, own_ref, chip_ref, cross_ref, cp_ref, member_out, coarse_out, down_out, up_out, ms, cs):
    odd = odd_ref[0] == 1
    chip = chip_ref[...].astype(F32)
    cross = cross_ref[...].astype(F32)
    low = low_lanes((HALF, 2 * CW))
    lead = jnp.where(odd, chip, cross)
    trail = jnp.where(odd, cross, chip)
    lead = [jnp.where(low, lead, 0.0), jnp.where(low, turn(lead), 0.0)]
    trail = [jnp.where(low, 0.0, turn(trail)), jnp.where(low, 0.0, trail)]
    lead = jnp.concatenate(lead, axis=0)
    trail = jnp.concatenate(trail, axis=0)
    for i in range(LV):
        rows = slice(i * MB, (i + 1) * MB)
        ms[i, :, : 2 * CW] = own_ref[rows, : 2 * CW] + lead[rows]
        ms[i, :, 2 * CW :] = own_ref[rows, 2 * CW :] + trail[rows]
        row = slice(LV * MB + i, LV * MB + i + 1)
        pert = cp_ref[i].astype(F32)
        cs[i, :, : 2 * CW] = pert[:, : 2 * CW] * (own_ref[row, : 2 * CW] + lead[row])
        cs[i, :, 2 * CW :] = pert[:, 2 * CW :] * (own_ref[row, 2 * CW :] + trail[row])
    for j in range(WL):
        member = None
        for i in range(max(0, j - 2 * HB), min(LV - 1, j) + 1):
            m, c = band_ref[i, j] * ms[i], band_ref[i, j] * cs[i]
            member, coarse = (m, c) if member is None else (member + m, coarse + c)
        if j < HB:
            down_out[j, :MB] = member.astype(BF16)
            down_out[j, MB:] = coarse.astype(BF16)
        elif j < HB + LV:
            member_out[j - HB] = member
            coarse_out[j - HB] = coarse
        else:
            up_out[j - HB - LV, :MB] = member.astype(BF16)
            up_out[j - HB - LV, MB:] = coarse.astype(BF16)


def finish_kernel(member_ref, coarse_ref, below_ref, above_ref, member_out, coarse_out):
    member_out[HB : LV - HB] = member_ref[HB : LV - HB]
    coarse_out[HB : LV - HB] = coarse_ref[HB : LV - HB]
    for j in range(HB):
        member_out[j] = member_ref[j] + below_ref[j, :MB].astype(F32)
        coarse_out[j] = coarse_ref[j] + below_ref[j, MB:].astype(F32)
        k = LV - HB + j
        member_out[k] = member_ref[k] + above_ref[j, :MB].astype(F32)
        coarse_out[k] = coarse_ref[k] + above_ref[j, MB:].astype(F32)


def shape(dims, kind):
    return jax.ShapeDtypeStruct(dims, kind)


PARAMS = pltpu.CompilerParams(vmem_limit_bytes=24 * 1024 * 1024)


def near(*values):
    return [pltpu.with_memory_space_constraint(value, pltpu.VMEM) for value in values]


def far(*values):
    return [pltpu.with_memory_space_constraint(value, pltpu.HBM) for value in values]


def shards(members_pert, coarse_pert, member_ctrl, coarse_ctrl, vert_loc, stencil, interp_w):
    tiles = lax.axis_size("tile")
    levs = lax.axis_size("lev")
    rising = [(i, i + 1) for i in range(levs - 1)]
    falling = [(j, i) for i, j in rising]
    on_chip = [(i, i ^ 1) for i in range(tiles)]
    off_chip = [(i, (i + 1) % tiles if i % 2 else (i - 1) % tiles) for i in range(tiles)]
    odd = (lax.axis_index("tile") % 2).astype(jnp.int32).reshape(1)
    first_level = lax.axis_index("lev") * LV
    padded = jnp.pad(vert_loc, ((0, 0), (HB, HB)))
    band = lax.dynamic_slice(padded, (first_level, first_level), (LV, WL))

    edge = pltpu.VMEM((HB, MB + CM, ND), BF16)
    held = [pltpu.VMEM(x.shape, x.dtype) for x in (member_ctrl, coarse_ctrl, coarse_pert, stencil, interp_w)]
    hbm = pl.BlockSpec(memory_space=pltpu.HBM)
    top, bottom, member_ctrl, coarse_ctrl, coarse_pert, stencil, interp_w = pl.pallas_call(
        gather_kernel,
        out_shape=(edge, edge, *held),
        in_specs=[hbm] * 5,
        out_specs=(VMEM,) * 7,
        scratch_shapes=[pltpu.SemaphoreType.DMA((9,))],
        compiler_params=PARAMS,
        name="gather",
    )(*far(member_ctrl, coarse_ctrl, coarse_pert, stencil, interp_w))
    below = lax.ppermute(top, "lev", rising)
    above = lax.ppermute(bottom, "lev", falling)
    matrix, pert = pl.pallas_call(
        weights_kernel,
        out_shape=(pltpu.VMEM((SPAN, NF), BF16), pltpu.VMEM((LV * MB, NF), BF16)),
        in_specs=[SMEM, VMEM, VMEM, hbm],
        out_specs=(VMEM, VMEM),
        scratch_shapes=[pltpu.SemaphoreType.DMA],
        cost_estimate=pl.CostEstimate(flops=16 * SPAN * NF, bytes_accessed=2 * SPAN * NF, transcendentals=0),
        compiler_params=PARAMS,
        name="weights",
    )(odd, *near(stencil, interp_w), *far(members_pert.reshape(LV * MB, NF)))
    packed = pltpu.VMEM((HALF, 2 * CW), BF16)
    own, chip, cross = pl.pallas_call(
        localize_kernel,
        out_shape=(pltpu.VMEM((ROWS, ND), BF16), packed, packed),
        in_specs=[SMEM, SMEM, VMEM, VMEM, VMEM, VMEM, VMEM],
        out_specs=(VMEM, VMEM, VMEM),
        scratch_shapes=[pltpu.VMEM((WL, MB, ND), F32), pltpu.VMEM((WL, CM, ND), F32), pltpu.VMEM((2 * HALF, ND), F32)],
        compiler_params=PARAMS,
        name="localize",
    )(odd, band, *near(member_ctrl, coarse_ctrl, below, above, coarse_pert))
    cross = lax.ppermute(cross, "tile", off_chip)
    chip = lax.ppermute(chip, "tile", on_chip)
    own, chip, cross = pl.pallas_call(
        fine_kernel,
        out_shape=(pltpu.VMEM((ROWS, ND), F32), packed, packed),
        in_specs=[VMEM] * 5,
        out_specs=(VMEM, VMEM, VMEM),
        scratch_shapes=[pltpu.VMEM((ROWS, SPAN), BF16)],
        compiler_params=PARAMS,
        name="fine",
    )(*near(own, chip, cross, matrix, pert))
    cross = lax.ppermute(cross, "tile", off_chip)
    chip = lax.ppermute(chip, "tile", on_chip)
    halo = pltpu.VMEM((HB, MB + CM, ND), BF16)
    finals = (shape((LV, MB, ND), F32), shape((LV, CM, ND), F32))
    member, coarse, down, up = pl.pallas_call(
        spread_kernel,
        out_shape=(pltpu.VMEM((LV, MB, ND), F32), pltpu.VMEM((LV, CM, ND), F32), halo, halo),
        in_specs=[SMEM, SMEM, VMEM, VMEM, VMEM, VMEM],
        out_specs=(VMEM, VMEM, VMEM, VMEM),
        scratch_shapes=[pltpu.VMEM((LV, MB, ND), F32), pltpu.VMEM((LV, CM, ND), F32)],
        compiler_params=PARAMS,
        name="spread",
    )(odd, band, *near(own, chip, cross, coarse_pert))
    above = lax.ppermute(down, "lev", falling)
    below = lax.ppermute(up, "lev", rising)
    return pl.pallas_call(
        finish_kernel,
        out_shape=finals,
        in_specs=[VMEM, VMEM, VMEM, VMEM],
        out_specs=(VMEM, VMEM),
        compiler_params=PARAMS,
        name="finish",
    )(*near(member, coarse, below, above))


def solution(mesh):
    block = P("lev", None, "tile")
    in_specs = (block, block, block, block, P(), P(None, "tile"), P(None, "tile"))
    return jax.shard_map(shards, mesh=mesh, in_specs=in_specs, out_specs=(block, block), check_vma=False)
```

time: 81.1 us -> 62.4 us (0.77)
  waiting for transfers between devices: 18.7 us -> 7.33 us
  matrix products: 9.56 us -> 0 us
  Pallas kernels: 0 us -> 9.51 us
  local copies, waits for them, and re-layouts: 6.07 us -> 0.78 us
  other arithmetic: 3.43 us -> 0 us
  starting transfers between devices: 41.8 us -> 43.6 us
    ppermute x8, waiting for transfers between devices: 18.7 us -> 7.33 us  [the longest x1 3.43 us: shards(): above = lax.ppermute(down, 'lev', falling)]
    dot_general x4 -> x0, matrix products: 9.56 us -> none  [the longest x1 4.14 us: shards(): lax.dot_general(adjoint.reshape(level_rows * kinds, fine_cells), interp_m...]
    pallas_call x0 -> x6, Pallas kernels: none -> 9.51 us  [the longest x1 3.79 us: shards(): pl.pallas_call(fine_kernel, out_shape=(pltpu.VMEM((ROWS, ND), F32), packe...]
    unnamed x11 -> x0, local copies, waits for them, and re-layouts: 2.72 us -> none
    slice x10 -> x0, local copies, waits for them, and re-layouts: 2.41 us -> none  [the longest x1 1.1 us: shards(): interp_w[corner][None, :]]
    reduce_sum x2 -> x0, other arithmetic: 1.86 us -> none  [the longest x1 0.99 us: shards(): jnp.sum(pert_float * interp[:, :members], axis=1) + interp[:, members]]
    ppermute x8, starting transfers between devices: 41.8 us -> 43.6 us  [the longest x2 25.7 us: shards(): cross = lax.ppermute(cross, 'tile', off_chip)]
    another operation x2 -> x0, other arithmetic: 1.02 us -> none
  transfers between devices with their start and end apart: 8 -> 8, of which waited for: 6 -> 5; matrix products, arithmetic and copies ran while one was open for 3% -> 1% of each run, Pallas kernels for 0% -> 3%
where the time goes in v1:
time: 62.4 us; the launch traced here: 62 us
  starting transfers between devices  43.6 us (70%)
  Pallas kernels  9.51 us (15%)
  waiting for transfers between devices  7.33 us (12%)
  local copies, waits for them, and re-layouts  0.78 us (1%)
  between operations  0.75 us (1%)
    ppermute x2, starting transfers between devices, shards(): cross = lax.ppermute(cross, 'tile', off_chip)  25.7 us
    ppermute x1, starting transfers between devices, shards(): below = lax.ppermute(top, 'lev', rising)  4.28 us
    ppermute x1, starting transfers between devices, shards(): above = lax.ppermute(bottom, 'lev', falling)  3.92 us
    ppermute x2, starting transfers between devices, shards(): chip = lax.ppermute(chip, 'tile', on_chip)  3.84 us
    pallas_call x1, Pallas kernels, shards(): pl.pallas_call(fine_kernel, out_shape=(pltpu.VMEM((ROWS, ND), F32), packe...  3.79 us
    ppermute x1, waiting for transfers between devices, shards(): above = lax.ppermute(down, 'lev', falling)  3.43 us
    ppermute x1, starting transfers between devices, shards(): below = lax.ppermute(up, 'lev', rising)  3.42 us
    ppermute x1, starting transfers between devices, shards(): above = lax.ppermute(down, 'lev', falling)  2.42 us
  transfers between devices with their start and end apart: 8, of which 5 were waited for; matrix products, arithmetic and copies ran while one was open for 1% of the time, Pallas kernels for 3%

profile of v1, /device:TPU:64, one launch (start us, length us, event | category | flops | bytes accessed | tf_op | source)
XLA Modules:
  0.0 62.0 jit_solution(2298459451291772163)
XLA Ops:
  0.6 1.1 %gather.1 = (bf16[4,24,256]{2,1,0:T(8,128)(2,1)S(1)}, bf16[4,24,256]{2,1,0:T(8,128)(2,1)S(1)}, bf16[16,16,256]{2,1,0:T(8,128)(2,1)S(1)}, bf16[16,8,256]{2,1,0:T(...) custom-call(bf16[16,16,256]{2,1,0:T(8,128)(2,1)} %mc_hbm.1, ...), custom_call_target="tpu_custom_call" | custom-call | tf_op jit(solution)/shard_map/gather/pallas_call | solution.py:210
  1.8 4.3 %collective-permute-start = (bf16[4,24,256]{2,1,0:T(8,128)(2,1)S(1)}, bf16[4,24,256]{2,1,0:T(8,128)(2,1)S(1)}, u32[]{:S(2)}, u32[]{:S(2)}) collective-permute-start(bf16[4,24,256]{2,1,0:T(8,128)(2,1)S(1)} %get-tuple-element.23), channel_id=1, source_target_pairs={{0,1},{1,2},{2,3},{4,5},{5,6},{6,7},{8,9},{9,10},{10,11},{12,13},{... | collective-permute-start | bytes 147464 | tf_op jit(solution)/shard_map/ppermute | solution.py:219
  6.0 3.9 %collective-permute-start.1 = (bf16[4,24,256]{2,1,0:T(8,128)(2,1)S(1)}, bf16[4,24,256]{2,1,0:T(8,128)(2,1)S(1)}, u32[]{:S(2)}, u32[]{:S(2)}) collective-permute-start(bf16[4,24,256]{2,1,0:T(8,128)(2,1)S(1)} %get-tuple-element.24), channel_id=1, source_target_pairs={{1,0},{2,1},{3,2},{5,4},{6,5},{7,6},{9,8},{10,9},{11,10},{13,12},{... | collective-permute-start | bytes 147464 | tf_op jit(solution)/shard_map/ppermute | solution.py:220
  10.0 0.8 %pad_dynamic-slice_fusion.band_ref = f32[16,24]{1,0:T(8,128)S(1)} fusion(s32[]{:T(128)S(6)} %select_n.14, s32[]{:T(128)S(6)} %select_n.15, f32[64,64]{1,0:T(8,128)} %param.11), kind=kLoop, calls=%fused_computation | loop fusion | bytes 17928 | tf_op jit(solution)/shard_map/dynamic_slice | solution.py:205
  10.8 0.0 collective-permute-done.below_ref
  10.8 1.6 %collective-permute-done.1.above_ref = bf16[4,24,256]{2,1,0:T(8,128)(2,1)S(1)} collective-permute-done((bf16[4,24,256]{2,1,0:T(8,128)(2,1)S(1)}, bf16[4,24,256]{2,1,0:T(8,128)(2,1)S(1)}, u32[]{:S(2)}, u32[]{:S(2)}) %collective-permute-start.1) | collective-permute-done | bytes 49184 | tf_op jit(solution)/shard_map/ppermute | solution.py:220
  12.4 1.0 %localize.1 = (bf16[272,256]{1,0:T(8,128)(2,1)S(1)}, bf16[144,128]{1,0:T(8,128)(2,1)S(1)}, bf16[144,128]{1,0:T(8,128)(2,1)S(1)}) custom-call(s32[1]{0:T(128)} %bitcast.odd_ref, f32[16,24]{1,0:T(8,128)S(1)} %pad_dynamic-slice_fusion.band_ref, bf16[16,16,256]{2,1,0:T(8,128)(2,1)S(1)} %get-tuple-element.21.mc_ref, ...), custom_call_target="tpu_custom_call" | custom-call | tf_op jit(solution)/shard_map/localize/pallas_call | solution.py:232
  13.4 1.9 %collective-permute-start.2 = (bf16[144,128]{1,0:T(8,128)(2,1)S(1)}, bf16[144,128]{1,0:T(8,128)(2,1)S(1)}, u32[]{:S(2)}, u32[]{:S(2)}) collective-permute-start(bf16[144,128]{1,0:T(8,128)(2,1)S(1)} %get-tuple-element.27), channel_id=1, source_target_pairs={{0,4},{4,0},{8,12},{12,8},{16,20},{20,16},{24,28},{28,24},{32,36},... | collective-permute-start | bytes 110600 | tf_op jit(solution)/shard_map/ppermute | solution.py:242
  15.3 14.0 %collective-permute-start.3 = (bf16[144,128]{1,0:T(8,128)(2,1)S(1)}, bf16[144,128]{1,0:T(8,128)(2,1)S(1)}, u32[]{:S(2)}, u32[]{:S(2)}) collective-permute-start(bf16[144,128]{1,0:T(8,128)(2,1)S(1)} %get-tuple-element.28), channel_id=1, source_target_pairs={{0,508},{4,8},{8,4},{12,16},{16,12},{20,24},{24,20},{28,32},{32,28... | collective-permute-start | bytes 110600 | tf_op jit(solution)/shard_map/ppermute | solution.py:241
  29.3 1.8 %weights.1 = (bf16[384,4096]{1,0:T(8,128)(2,1)S(1)}, bf16[256,4096]{1,0:T(8,128)(2,1)S(1)}) custom-call(s32[1]{0:T(128)} %bitcast.odd_ref, s32[4,4096]{1,0:T(4,128)S(1)} %get-tuple-element.29.stencil_ref, bf16[4,4096]{1,0:T(4,128)(2,1)S(1)} %get-tuple-element.30.weight_ref, bf16[256,4096]{1,0:T(8,128)(2,1)} %bitcast.2), custom_call_target="tpu_custom_call" | custom-call | flops 25165824 | bytes 3145728 | tf_op jit(solution)/shard_map/weights/pallas_call | solution.py:221
  31.1 0.0 collective-permute-done.2.chip_ref
  31.2 0.1 collective-permute-done.3.cross_ref
  31.3 3.8 %fine.1 = (f32[272,256]{1,0:T(8,128)S(1)}, bf16[144,128]{1,0:T(8,128)(2,1)S(1)}, bf16[144,128]{1,0:T(8,128)(2,1)S(1)}) custom-call(bf16[272,256]{1,0:T(8,128)(2,1)S(1)} %get-tuple-element.26.own_ref, bf16[144,128]{1,0:T(8,128)(2,1)S(1)} %collective-permute-done.2.chip_ref, bf16[144,128]{1,0:T(8,128)(2,1)S(1)} %collective-permute-done.3.cross_ref, ...), custom_call_target="tpu_custom_call" | custom-call | tf_op jit(solution)/shard_map/fine/pallas_call | solution.py:243
  35.1 1.9 %collective-permute-start.4 = (bf16[144,128]{1,0:T(8,128)(2,1)S(1)}, bf16[144,128]{1,0:T(8,128)(2,1)S(1)}, u32[]{:S(2)}, u32[]{:S(2)}) collective-permute-start(bf16[144,128]{1,0:T(8,128)(2,1)S(1)} %get-tuple-element.34), channel_id=1, source_target_pairs={{0,4},{4,0},{8,12},{12,8},{16,20},{20,16},{24,28},{28,24},{32,36},... | collective-permute-start | bytes 110600 | tf_op jit(solution)/shard_map/ppermute | solution.py:253
  37.0 11.8 %collective-permute-start.5 = (bf16[144,128]{1,0:T(8,128)(2,1)S(1)}, bf16[144,128]{1,0:T(8,128)(2,1)S(1)}, u32[]{:S(2)}, u32[]{:S(2)}) collective-permute-start(bf16[144,128]{1,0:T(8,128)(2,1)S(1)} %get-tuple-element.35), channel_id=1, source_target_pairs={{0,508},{4,8},{8,4},{12,16},{16,12},{20,24},{24,20},{28,32},{32,28... | collective-permute-start | bytes 110600 | tf_op jit(solution)/shard_map/ppermute | solution.py:252
  48.8 0.0 collective-permute-done.4.chip_ref
  48.8 2.0 %collective-permute-done.5.cross_ref = bf16[144,128]{1,0:T(8,128)(2,1)S(1)} collective-permute-done((bf16[144,128]{1,0:T(8,128)(2,1)S(1)}, bf16[144,128]{1,0:T(8,128)(2,1)S(1)}, u32[]{:S(2)}, u32[]{:S(2)}) %collective-permute-start.5) | collective-permute-done | bytes 36896 | tf_op jit(solution)/shard_map/ppermute | solution.py:252
  50.8 1.0 %spread.1 = (f32[16,16,256]{2,1,0:T(8,128)S(1)}, f32[16,8,256]{2,1,0:T(8,128)S(1)}, bf16[4,24,256]{2,1,0:T(8,128)(2,1)S(1)}, bf16[4,24,256]{2,1,0:T(8,128)(2,1)S(1)}) custom-call(s32[1]{0:T(128)} %bitcast.odd_ref, f32[16,24]{1,0:T(8,128)S(1)} %pad_dynamic-slice_fusion.band_ref, f32[272,256]{1,0:T(8,128)S(1)} %get-tuple-element.33.own_ref, ...), custom_call_target="tpu_custom_call" | custom-call | tf_op jit(solution)/shard_map/spread/pallas_call | solution.py:256
  51.8 3.4 %collective-permute-start.6 = (bf16[4,24,256]{2,1,0:T(8,128)(2,1)S(1)}, bf16[4,24,256]{2,1,0:T(8,128)(2,1)S(1)}, u32[]{:S(2)}, u32[]{:S(2)}) collective-permute-start(bf16[4,24,256]{2,1,0:T(8,128)(2,1)S(1)} %get-tuple-element.38), channel_id=1, source_target_pairs={{0,1},{1,2},{2,3},{4,5},{5,6},{6,7},{8,9},{9,10},{10,11},{12,13},{... | collective-permute-start | bytes 147464 | tf_op jit(solution)/shard_map/ppermute | solution.py:266
  55.2 2.4 %collective-permute-start.7 = (bf16[4,24,256]{2,1,0:T(8,128)(2,1)S(1)}, bf16[4,24,256]{2,1,0:T(8,128)(2,1)S(1)}, u32[]{:S(2)}, u32[]{:S(2)}) collective-permute-start(bf16[4,24,256]{2,1,0:T(8,128)(2,1)S(1)} %get-tuple-element.39), channel_id=1, source_target_pairs={{1,0},{2,1},{3,2},{5,4},{6,5},{7,6},{9,8},{10,9},{11,10},{13,12},{... | collective-permute-start | bytes 147464 | tf_op jit(solution)/shard_map/ppermute | solution.py:265
  57.7 0.1 collective-permute-done.6.below_ref
  57.8 3.4 %collective-permute-done.7.above_ref = bf16[4,24,256]{2,1,0:T(8,128)(2,1)S(1)} collective-permute-done((bf16[4,24,256]{2,1,0:T(8,128)(2,1)S(1)}, bf16[4,24,256]{2,1,0:T(8,128)(2,1)S(1)}, u32[]{:S(2)}, u32[]{:S(2)}) %collective-permute-start.7) | collective-permute-done | bytes 49184 | tf_op jit(solution)/shard_map/ppermute | solution.py:265
  61.2 0.8 %finish.1 = (f32[16,16,256]{2,1,0:T(8,128)}, f32[16,8,256]{2,1,0:T(8,128)}) custom-call(f32[16,16,256]{2,1,0:T(8,128)S(1)} %get-tuple-element.36.member_ref, f32[16,8,256]{2,1,0:T(8,128)S(1)} %get-tuple-element.37.coarse_ref, bf16[4,24,256]{2,1,0:T(8,128)(2,1)S(1)} %collective-permute-done.6.below_ref, bf16[4,24,256]{2,1,0:T(8,128)(2,1)S(1)} %collective-permute-done.7.above_ref), custom_call_target="tpu_custom_call" | custom-call | tf_op jit(solution)/shard_map/finish/pallas_call | solution.py:267
Async XLA Ops:
  1.8 9.0 %collective-permute-start = (bf16[4,24,256]{2,1,0:T(8,128)(2,1)S(1)}, bf16[4,24,256]{2,1,0:T(8,128)(2,1)S(1)}, u32[]{:S(2)}, u32[]{:S(2)}) collective-permute-start(bf16[4,24,256]{2,1,0:T(8,128)(2,1)S(1)} %get-tuple-element.23), channel_id=1, source_target_pairs={{0,1},{1,2},{2,3},{4,5},{5,6},{6,7},{8,9},{9,10},{10,11},{12,13},{... | collective-permute-start | bytes 147464 | tf_op jit(solution)/shard_map/ppermute | solution.py:219
  6.0 6.3 %collective-permute-start.1 = (bf16[4,24,256]{2,1,0:T(8,128)(2,1)S(1)}, bf16[4,24,256]{2,1,0:T(8,128)(2,1)S(1)}, u32[]{:S(2)}, u32[]{:S(2)}) collective-permute-start(bf16[4,24,256]{2,1,0:T(8,128)(2,1)S(1)} %get-tuple-element.24), channel_id=1, source_target_pairs={{1,0},{2,1},{3,2},{5,4},{6,5},{7,6},{9,8},{10,9},{11,10},{13,12},{... | collective-permute-start | bytes 147464 | tf_op jit(solution)/shard_map/ppermute | solution.py:220
  13.4 17.7 %collective-permute-start.2 = (bf16[144,128]{1,0:T(8,128)(2,1)S(1)}, bf16[144,128]{1,0:T(8,128)(2,1)S(1)}, u32[]{:S(2)}, u32[]{:S(2)}) collective-permute-start(bf16[144,128]{1,0:T(8,128)(2,1)S(1)} %get-tuple-element.27), channel_id=1, source_target_pairs={{0,4},{4,0},{8,12},{12,8},{16,20},{20,16},{24,28},{28,24},{32,36},... | collective-permute-start | bytes 110600 | tf_op jit(solution)/shard_map/ppermute | solution.py:242
  15.3 16.0 %collective-permute-start.3 = (bf16[144,128]{1,0:T(8,128)(2,1)S(1)}, bf16[144,128]{1,0:T(8,128)(2,1)S(1)}, u32[]{:S(2)}, u32[]{:S(2)}) collective-permute-start(bf16[144,128]{1,0:T(8,128)(2,1)S(1)} %get-tuple-element.28), channel_id=1, source_target_pairs={{0,508},{4,8},{8,4},{12,16},{16,12},{20,24},{24,20},{28,32},{32,28... | collective-permute-start | bytes 110600 | tf_op jit(solution)/shard_map/ppermute | solution.py:241
  35.1 13.7 %collective-permute-start.4 = (bf16[144,128]{1,0:T(8,128)(2,1)S(1)}, bf16[144,128]{1,0:T(8,128)(2,1)S(1)}, u32[]{:S(2)}, u32[]{:S(2)}) collective-permute-start(bf16[144,128]{1,0:T(8,128)(2,1)S(1)} %get-tuple-element.34), channel_id=1, source_target_pairs={{0,4},{4,0},{8,12},{12,8},{16,20},{20,16},{24,28},{28,24},{32,36},... | collective-permute-start | bytes 110600 | tf_op jit(solution)/shard_map/ppermute | solution.py:253
  37.0 13.8 %collective-permute-start.5 = (bf16[144,128]{1,0:T(8,128)(2,1)S(1)}, bf16[144,128]{1,0:T(8,128)(2,1)S(1)}, u32[]{:S(2)}, u32[]{:S(2)}) collective-permute-start(bf16[144,128]{1,0:T(8,128)(2,1)S(1)} %get-tuple-element.35), channel_id=1, source_target_pairs={{0,508},{4,8},{8,4},{12,16},{16,12},{20,24},{24,20},{28,32},{32,28... | collective-permute-start | bytes 110600 | tf_op jit(solution)/shard_map/ppermute | solution.py:252
  51.8 6.0 %collective-permute-start.6 = (bf16[4,24,256]{2,1,0:T(8,128)(2,1)S(1)}, bf16[4,24,256]{2,1,0:T(8,128)(2,1)S(1)}, u32[]{:S(2)}, u32[]{:S(2)}) collective-permute-start(bf16[4,24,256]{2,1,0:T(8,128)(2,1)S(1)} %get-tuple-element.38), channel_id=1, source_target_pairs={{0,1},{1,2},{2,3},{4,5},{5,6},{6,7},{8,9},{9,10},{10,11},{12,13},{... | collective-permute-start | bytes 147464 | tf_op jit(solution)/shard_map/ppermute | solution.py:266
  55.2 6.0 %collective-permute-start.7 = (bf16[4,24,256]{2,1,0:T(8,128)(2,1)S(1)}, bf16[4,24,256]{2,1,0:T(8,128)(2,1)S(1)}, u32[]{:S(2)}, u32[]{:S(2)}) collective-permute-start(bf16[4,24,256]{2,1,0:T(8,128)(2,1)S(1)} %get-tuple-element.39), channel_id=1, source_target_pairs={{1,0},{2,1},{3,2},{5,4},{6,5},{7,6},{9,8},{10,9},{11,10},{13,12},{... | collective-permute-start | bytes 147464 | tf_op jit(solution)/shard_map/ppermute | solution.py:265

commit v2 on v1

v2 whole, which is shorter than its diff:
```python
import jax
import jax.numpy as jnp
from jax import lax
from jax.experimental import pallas as pl
from jax.experimental.pallas import tpu as pltpu
from jax.sharding import PartitionSpec as P


HB = 4
CW = 64
LV = 16
MB = 16
CM = 8
ND = 256
NF = 4096
WL = LV + 2 * HB
LEVS = 4
BAND = 2 * HB + 1
ROWS = LV * MB + LV
HALF = 144
SPAN = ND + 2 * CW
BLOCK = 512
STEP = 2048
F32 = jnp.float32
BF16 = jnp.bfloat16
VMEM = pl.BlockSpec(memory_space=pltpu.VMEM)


def low_lanes(shape):
    return lax.broadcasted_iota(jnp.int32, shape, 1) < CW


def odd_tile():
    return lax.axis_index("tile") % 2


def odd_lev():
    return lax.axis_index("lev") % 2


def second_half():
    tile = lax.axis_index("tile")
    middle = (tile + 1) // 2 == lax.axis_size("tile") // 4
    return jnp.where(middle, tile % 2, 1 - tile % 2)


def turn(value):
    return pltpu.roll(value, CW, 1)


def run_copies(moves, sems):
    copies = [pltpu.make_async_copy(source, target, sems.at[k]) for k, (source, target) in enumerate(moves)]
    for copy in copies:
        copy.start()
    return copies


def edges_kernel(mc_hbm, cc_hbm, cp_hbm, outer, inner, sems):
    near_first = odd_lev() * (LV - HB)
    far_first = LV - HB - near_first
    moves = []
    for first, target in ((near_first, inner), (far_first, outer)):
        moves.append((mc_hbm.at[pl.ds(first, HB)], target.at[:, pl.ds(0, MB)]))
        moves.append((cc_hbm.at[pl.ds(first, HB)], target.at[:, pl.ds(MB, CM)]))
        moves.append((cp_hbm.at[pl.ds(first, HB)], target.at[:, pl.ds(MB + CM, CM)]))
    for copy in run_copies(moves, sems):
        copy.wait()


def load_kernel(vert_hbm, mc_hbm, cc_hbm, cp_hbm, stencil_hbm, weight_hbm, pert_hbm, ahead_ref, back_ref, mc, cc, cp, stencil, weight, pert, vert, sems):
    moves = [(vert_hbm, vert), (mc_hbm, mc), (cc_hbm, cc), (cp_hbm, cp), (stencil_hbm, stencil), (weight_hbm, weight), (pert_hbm, pert)]
    copies = run_copies(moves, sems)
    first = lax.axis_index("lev") * LV
    final = LV * lax.axis_size("lev") - 1
    copies[0].wait()
    for i in range(LV):
        for d in range(BAND):
            near = first + i
            other = first + i + d - HB
            if i + d < HB:
                other = jnp.maximum(other, 0)
            elif i + d >= HB + LV:
                other = jnp.minimum(other, final)
            ahead_ref[i, d] = jnp.full((8, 128), vert[near, other], F32)
            back_ref[i, d] = jnp.full((8, 128), vert[other, near], F32)
    for copy in copies[1:]:
        copy.wait()


def localize_kernel(band_ref, mc_ref, cc_ref, outer_ref, inner_ref, cp_ref, own_ref, chip_ref, cross_ref, ms, cs, full):
    swapped = odd_lev() == 1
    for j in range(HB):
        outer = outer_ref[j, : MB + CM].astype(F32)
        inner = inner_ref[j, : MB + CM].astype(F32)
        below = jnp.where(swapped, outer, inner)
        above = jnp.where(swapped, inner, outer)
        ms[j], cs[j] = below[:MB], below[MB:]
        ms[HB + LV + j], cs[HB + LV + j] = above[:MB], above[MB:]
    for j in range(LV):
        ms[HB + j] = mc_ref[j].astype(F32)
        cs[HB + j] = cc_ref[j].astype(F32)
    full[ROWS:] = jnp.zeros((2 * HALF - ROWS, ND), F32)
    for i in range(LV):
        member = scaled(band_ref[i, 0], ms[i])
        coarse = scaled(band_ref[i, 0], cs[i])
        for d in range(1, BAND):
            member = member + scaled(band_ref[i, d], ms[i + d])
            coarse = coarse + scaled(band_ref[i, d], cs[i + d])
        full[i * MB : (i + 1) * MB] = member
        coarse = coarse.astype(BF16).astype(F32)
        full[LV * MB + i : LV * MB + i + 1] = jnp.sum(cp_ref[i].astype(F32) * coarse, axis=0, keepdims=True)
    own_ref[...] = full[:ROWS].astype(BF16)
    odd = odd_tile() == 1
    first = full[:, : 2 * CW]
    last = full[:, ND - 2 * CW :]
    low = low_lanes((HALF, 2 * CW))
    first = jnp.where(low, first[:HALF], turn(first[HALF:]))
    last = jnp.where(low, turn(last[:HALF]), last[HALF:])
    cross_ref[...] = jnp.where(odd, last, first).astype(BF16)
    chip_ref[...] = jnp.where(odd, first, last).astype(BF16)


def weights_kernel(stencil_ref, weight_ref, out_ref):
    odd = odd_tile()
    rows = 16
    zero = jnp.zeros((rows, BLOCK), BF16)
    for start in range(0, NF, BLOCK):
        span = pl.ds(start, BLOCK)
        row = lax.broadcasted_iota(jnp.int32, (rows, BLOCK), 0)
        cells = [jnp.broadcast_to(stencil_ref[q : q + 1, span], (rows, BLOCK)) - row for q in range(4)]
        weights = [jnp.broadcast_to(weight_ref[q : q + 1, span].astype(F32), (rows, BLOCK)).astype(BF16) for q in range(4)]
        for low, high, first in ((0, ND, CW), (ND, ND + CW, (1 - odd) * (ND + CW)), (ND + CW, SPAN, odd * (ND + CW))):
            inside = [(cell - first).astype(jnp.int16) for cell in cells]
            for base in range(low, high, rows):
                value = jnp.where(inside[0] == jnp.int16(base - low), weights[0], zero)
                for q in range(1, 4):
                    value = jnp.where(inside[q] == jnp.int16(base - low), weights[q], value)
                out_ref[base : base + rows, span] = value


def scaled(factor, value):
    rows, lanes = value.shape
    return jnp.tile(factor, (rows // 8, lanes // 128)) * value


def fine_kernel(own_ref, chip_ref, cross_ref, matrix_ref, pert, own_out, chip_out, cross_out, field):
    chip = chip_ref[...].astype(F32)
    cross = cross_ref[...].astype(F32)
    low = low_lanes((HALF, 2 * CW))
    field[:, :ND] = own_ref[...]
    field[:HALF, ND:] = jnp.where(low, chip, turn(cross)).astype(BF16)
    field[HALF:, ND:] = jnp.where(low, turn(chip), cross)[: ROWS - HALF].astype(BF16)
    total = jnp.zeros((ROWS, SPAN), F32)
    for b in range(NF // STEP):
        span = pl.ds(b * STEP, STEP)
        matrix = matrix_ref[:, span]
        interp = jnp.dot(field[...], matrix, preferred_element_type=F32)
        member = pert[:, span].astype(F32).reshape(LV, MB, STEP)
        increment = jnp.sum(member * interp[: LV * MB].reshape(LV, MB, STEP), axis=1) + interp[LV * MB :]
        adjoint = (member * increment[:, None, :]).astype(BF16).reshape(LV * MB, STEP)
        adjoint = jnp.concatenate([adjoint, increment.astype(BF16)], axis=0)
        total = total + lax.dot_general(adjoint, matrix, (((1,), (1,)), ((), ())), preferred_element_type=F32)
    own_out[...] = total[:, :ND]
    top = total[:HALF, ND:]
    bottom = jnp.concatenate([total[HALF:, ND:], jnp.zeros((2 * HALF - ROWS, 2 * CW), F32)], axis=0)
    chip_out[...] = jnp.where(low, top, turn(bottom)).astype(BF16)
    cross_out[...] = jnp.where(low, turn(top), bottom).astype(BF16)


def joined(chunk, odd):
    chunk = chunk.astype(F32)
    turned = turn(chunk)
    low = low_lanes((HALF, 2 * CW))
    lead = jnp.concatenate([jnp.where(low, chunk, 0.0), jnp.where(low, turned, 0.0)], axis=0)
    trail = jnp.concatenate([jnp.where(low, 0.0, turned), jnp.where(low, 0.0, chunk)], axis=0)
    return jnp.where(odd, 0.0, lead), jnp.where(odd, trail, 0.0)


def merge_kernel(own_ref, chip_ref, cross_ref, own_out, send_ref):
    here = second_half() * LEVS
    there = LEVS - here
    lev = lax.axis_index("lev")
    for k in range(LEVS):
        send_ref[there + k] = cross_ref[...]
    lead, trail = joined(chip_ref[...], odd_tile() == 0)
    own_out[:, : 2 * CW] = own_ref[:, : 2 * CW] + lead[:ROWS]
    own_out[:, 2 * CW :] = own_ref[:, 2 * CW :] + trail[:ROWS]
    edge = HB * MB
    blank = jnp.zeros((HALF - 2 * edge - 2 * HB, 2 * CW), F32)
    for first, place in ((0, jnp.maximum(lev - 1, 0)), (LV - HB, jnp.minimum(lev + 1, LEVS - 1))):
        rows = slice(first * MB, first * MB + edge)
        row = slice(LV * MB + first, LV * MB + first + HB)
        parts = [own_out[rows, : 2 * CW], own_out[rows, 2 * CW :], own_out[row, : 2 * CW], own_out[row, 2 * CW :], blank]
        send_ref[here + place] = jnp.concatenate(parts, axis=0).astype(BF16)


def finish_kernel(band_ref, own_ref, got_ref, cp_ref, outer_ref, inner_ref, member_hbm, coarse_hbm, ms, cs, member_out, coarse_out, sems):
    odd = odd_tile() == 1
    swapped = odd_lev() == 1
    here = second_half() * LEVS
    there = LEVS - here
    lev = lax.axis_index("lev")
    lower = jnp.maximum(lev - 1, 0)
    upper = jnp.minimum(lev + 1, LEVS - 1)
    wide = 2 * CW
    edge = HB * MB
    lead, trail = joined(got_ref[there + lev], odd)
    for i in range(LV):
        rows = slice(i * MB, (i + 1) * MB)
        row = slice(LV * MB + i, LV * MB + i + 1)
        ms[HB + i, :, :wide] = own_ref[rows, :wide] + lead[rows]
        ms[HB + i, :, wide:] = own_ref[rows, wide:] + trail[rows]
        pert = cp_ref[i].astype(F32)
        cs[HB + i, :, :wide] = pert[:, :wide] * (own_ref[row, :wide] + lead[row])
        cs[HB + i, :, wide:] = pert[:, wide:] * (own_ref[row, wide:] + trail[row])
    for place, first, base, below in ((lower, LV - HB, 0, swapped), (upper, 0, HB + LV, ~swapped)):
        lead, trail = joined(got_ref[there + place], odd)
        near = got_ref[here + place].astype(F32)
        near = jnp.where(place == lev, 0.0, near)
        lead = jnp.where(place == lev, 0.0, lead)
        trail = jnp.where(place == lev, 0.0, trail)
        for w in range(HB):
            rows = slice((first + w) * MB, (first + w + 1) * MB)
            row = slice(LV * MB + first + w, LV * MB + first + w + 1)
            ms[base + w, :, :wide] = near[w * MB : (w + 1) * MB] + lead[rows]
            ms[base + w, :, wide:] = near[edge + w * MB : edge + (w + 1) * MB] + trail[rows]
            pert = jnp.where(below, outer_ref[w, MB + CM :].astype(F32), inner_ref[w, MB + CM :].astype(F32))
            k = 2 * edge + w
            cs[base + w, :, :wide] = pert[:, :wide] * (near[k : k + 1] + lead[row])
            cs[base + w, :, wide:] = pert[:, wide:] * (near[k + HB : k + HB + 1] + trail[row])
    copies = []
    for j in range(LV):
        member = scaled(band_ref[j, 0], ms[j])
        coarse = scaled(band_ref[j, 0], cs[j])
        for d in range(1, BAND):
            member = member + scaled(band_ref[j, d], ms[j + d])
            coarse = coarse + scaled(band_ref[j, d], cs[j + d])
        member_out[j] = member
        coarse_out[j] = coarse
        if j % HB == HB - 1:
            span = pl.ds(j + 1 - HB, HB)
            for source, target in ((member_out, member_hbm), (coarse_out, coarse_hbm)):
                copies.append(pltpu.make_async_copy(source.at[span], target.at[span], sems.at[len(copies)]))
                copies[-1].start()
    for copy in copies:
        copy.wait()


def shape(dims, kind):
    return jax.ShapeDtypeStruct(dims, kind)


PARAMS = pltpu.CompilerParams(vmem_limit_bytes=24 * 1024 * 1024)


def near(*values):
    return [pltpu.with_memory_space_constraint(value, pltpu.VMEM) for value in values]


def far(*values):
    return [pltpu.with_memory_space_constraint(value, pltpu.HBM) for value in values]


def shards(members_pert, coarse_pert, member_ctrl, coarse_ctrl, vert_loc, stencil, interp_w):
    tiles = lax.axis_size("tile")
    levs = lax.axis_size("lev")
    outer_pairs = [(i, i ^ 1) for i in range(levs)]
    inner_pairs = [(1, 2), (2, 1)]
    on_chip = [(i, i ^ 1) for i in range(tiles)]
    off_chip = [(i, (i + 1) % tiles if i % 2 else (i - 1) % tiles) for i in range(tiles)]
    edge = pltpu.VMEM((HB, MB + 2 * CM, ND), BF16)
    hbm = pl.BlockSpec(memory_space=pltpu.HBM)
    outer, inner = pl.pallas_call(
        edges_kernel,
        out_shape=(edge, edge),
        in_specs=[hbm] * 3,
        out_specs=(VMEM, VMEM),
        scratch_shapes=[pltpu.SemaphoreType.DMA((6,))],
        compiler_params=PARAMS,
        name="edges",
    )(*far(member_ctrl, coarse_ctrl, coarse_pert))
    inner = lax.ppermute(inner, "lev", inner_pairs)
    outer = lax.ppermute(outer, "lev", outer_pairs)
    splats = pltpu.VMEM((LV, BAND, 8, 128), F32)
    values = (member_ctrl, coarse_ctrl, coarse_pert, stencil, interp_w, members_pert.reshape(LV * MB, NF))
    ahead, back, member_ctrl, coarse_ctrl, coarse_pert, stencil, interp_w, pert = pl.pallas_call(
        load_kernel,
        out_shape=(splats, splats, *[pltpu.VMEM(x.shape, x.dtype) for x in values]),
        in_specs=[hbm] * 7,
        out_specs=(VMEM,) * 8,
        scratch_shapes=[pltpu.SMEM(vert_loc.shape, F32), pltpu.SemaphoreType.DMA((7,))],
        compiler_params=PARAMS,
        name="load",
    )(*far(vert_loc, *values))
    matrix = pl.pallas_call(
        weights_kernel,
        out_shape=pltpu.VMEM((SPAN, NF), BF16),
        in_specs=[VMEM, VMEM],
        out_specs=VMEM,
        cost_estimate=pl.CostEstimate(flops=16 * SPAN * NF, bytes_accessed=2 * SPAN * NF, transcendentals=0),
        compiler_params=PARAMS,
        name="weights",
    )(*near(stencil, interp_w))
    packed = pltpu.VMEM((HALF, 2 * CW), BF16)
    own, chip, cross = pl.pallas_call(
        localize_kernel,
        out_shape=(pltpu.VMEM((ROWS, ND), BF16), packed, packed),
        in_specs=[VMEM] * 6,
        out_specs=(VMEM, VMEM, VMEM),
        scratch_shapes=[pltpu.VMEM((WL, MB, ND), F32), pltpu.VMEM((WL, CM, ND), F32), pltpu.VMEM((2 * HALF, ND), F32)],
        compiler_params=PARAMS,
        name="localize",
    )(*near(ahead, member_ctrl, coarse_ctrl, outer, inner, coarse_pert))
    cross = lax.ppermute(cross, "tile", off_chip)
    chip = lax.ppermute(chip, "tile", on_chip)
    own, chip, cross = pl.pallas_call(
        fine_kernel,
        out_shape=(pltpu.VMEM((ROWS, ND), F32), packed, packed),
        in_specs=[VMEM] * 5,
        out_specs=(VMEM, VMEM, VMEM),
        scratch_shapes=[pltpu.VMEM((ROWS, SPAN), BF16)],
        compiler_params=PARAMS,
        name="fine",
    )(*near(own, chip, cross, matrix, pert))
    chip = lax.ppermute(chip, "tile", on_chip)
    own, send = pl.pallas_call(
        merge_kernel,
        out_shape=(pltpu.VMEM((ROWS, ND), F32), pltpu.VMEM((2 * LEVS, HALF, 2 * CW), BF16)),
        in_specs=[VMEM, VMEM, VMEM],
        out_specs=(VMEM, VMEM),
        compiler_params=PARAMS,
        name="merge",
    )(*near(own, chip, cross))
    pairs = [(t, (t + 1) % tiles) if t + 1 != tiles // 2 else (t + 1, t) for t in range(1, tiles, 2)]
    groups = [[t * levs + z for t in pair for z in range(levs)] for pair in pairs]
    got = lax.all_to_all(send, ("tile", "lev"), 0, 0, axis_index_groups=groups)
    finals = (shape((LV, MB, ND), F32), shape((LV, CM, ND), F32))
    return pl.pallas_call(
        finish_kernel,
        out_shape=finals,
        in_specs=[VMEM] * 6,
        out_specs=(hbm, hbm),
        scratch_shapes=[
            pltpu.VMEM((WL, MB, ND), F32),
            pltpu.VMEM((WL, CM, ND), F32),
            pltpu.VMEM((LV, MB, ND), F32),
            pltpu.VMEM((LV, CM, ND), F32),
            pltpu.SemaphoreType.DMA((2 * LV // HB,)),
        ],
        compiler_params=PARAMS,
        name="finish",
    )(*near(back, own, got, coarse_pert, outer, inner))


def solution(mesh):
    block = P("lev", None, "tile")
    in_specs = (block, block, block, block, P(), P(None, "tile"), P(None, "tile"))
    return jax.shard_map(shards, mesh=mesh, in_specs=in_specs, out_specs=(block, block), check_vma=False)
```

time: 62.4 us -> 55.4 us (0.89)
  starting transfers between devices: 43.6 us -> 23.8 us
  blocking collectives: 0 us -> 17.8 us
  waiting for transfers between devices: 7.33 us -> 4.57 us
  Pallas kernels: 9.51 us -> 8.15 us
  local copies, waits for them, and re-layouts: 0.78 us -> 0 us
    all_to_all x0 -> x1, blocking collectives: none -> 17.8 us  [shards(): got = lax.all_to_all(send, ('tile', 'lev'), 0, 0, axis_index_groups=groups)]
    ppermute x2 -> x1, starting transfers between devices: 25.7 us -> 11.2 us  [shards(): cross = lax.ppermute(cross, 'tile', off_chip)]
    ppermute x4 -> x2, starting transfers between devices: 14 us -> 8.83 us  [the longest x1 6.91 us: shards(): outer = lax.ppermute(outer, 'lev', outer_pairs)]
    ppermute x4 -> x2, waiting for transfers between devices: 5.18 us -> 2.34 us  [the longest x1 2.34 us: shards(): inner = lax.ppermute(inner, 'lev', inner_pairs)]
    ppermute x2, waiting for transfers between devices: 0.01 us -> 1.18 us  [shards(): chip = lax.ppermute(chip, 'tile', on_chip)]
    ppermute x2 -> x1, waiting for transfers between devices: 2.14 us -> 1.05 us  [shards(): cross = lax.ppermute(cross, 'tile', off_chip)]
    pallas_call x1, Pallas kernels: 3.79 us -> 2.75 us  [shards(): pl.pallas_call(fine_kernel, out_shape=(pltpu.VMEM((ROWS, ND), F32), packe...]
    dynamic_slice x1 -> x0, local copies, waits for them, and re-layouts: 0.78 us -> none  [shards(): band = lax.dynamic_slice(padded, (first_level, first_level), (LV, WL))]
  transfers between devices with their start and end apart: 8 -> 5, of which waited for: 5 -> 3; matrix products, arithmetic and copies ran while one was open for 1% -> 0% of each run, Pallas kernels for 3% -> 6%
where the time goes in v2:
time: 55.4 us; the launch traced here: 55 us
  starting transfers between devices  23.8 us (43%)
  blocking collectives  17.8 us (32%)
  Pallas kernels  8.15 us (15%)
  waiting for transfers between devices  4.57 us (8%)
  between operations  0.72 us (1%)
    all_to_all x1, blocking collectives, shards(): got = lax.all_to_all(send, ('tile', 'lev'), 0, 0, axis_index_groups=groups)  17.8 us
    ppermute x1, starting transfers between devices, shards(): cross = lax.ppermute(cross, 'tile', off_chip)  11.2 us
    ppermute x1, starting transfers between devices, shards(): outer = lax.ppermute(outer, 'lev', outer_pairs)  6.91 us
    ppermute x2, starting transfers between devices, shards(): chip = lax.ppermute(chip, 'tile', on_chip)  3.84 us
    pallas_call x1, Pallas kernels, shards(): pl.pallas_call(fine_kernel, out_shape=(pltpu.VMEM((ROWS, ND), F32), packe...  2.75 us
    ppermute x1, waiting for transfers between devices, shards(): inner = lax.ppermute(inner, 'lev', inner_pairs)  2.34 us
    ppermute x1, starting transfers between devices, shards(): inner = lax.ppermute(inner, 'lev', inner_pairs)  1.92 us
    pallas_call x1, Pallas kernels, shards(): pl.pallas_call(load_kernel, out_shape=(splats, splats, *[pltpu.VMEM(x.sha...  1.88 us
  transfers between devices with their start and end apart: 5, of which 3 were waited for; matrix products, arithmetic and copies ran while one was open for 0% of the time, Pallas kernels for 6%

profile of v2, /device:TPU:64, one launch (start us, length us, event | category | flops | bytes accessed | tf_op | source)
XLA Modules:
  0.0 55.0 jit_solution(6447335890140170364)
XLA Ops:
  0.6 0.9 %edges.1 = (bf16[4,32,256]{2,1,0:T(8,128)(2,1)S(1)}, bf16[4,32,256]{2,1,0:T(8,128)(2,1)S(1)}) custom-call(bf16[16,16,256]{2,1,0:T(8,128)(2,1)} %mc_hbm.3, bf16[16,8,256]{2,1,0:T(8,128)(2,1)} %cc_hbm.3, bf16[16,8,256]{2,1,0:T(8,128)(2,1)} %cp_hbm.3), custom_call_target="tpu_custom_call" | custom-call | tf_op jit(solution)/shard_map/edges/pallas_call | solution.py:273
  1.5 6.9 %collective-permute-start = (bf16[4,32,256]{2,1,0:T(8,128)(2,1)S(1)}, bf16[4,32,256]{2,1,0:T(8,128)(2,1)S(1)}, u32[]{:S(2)}, u32[]{:S(2)}) collective-permute-start(bf16[4,32,256]{2,1,0:T(8,128)(2,1)S(1)} %get-tuple-element.24), channel_id=1, source_target_pairs={{0,1},{1,0},{2,3},{3,2},{4,5},{5,4},{6,7},{7,6},{8,9},{9,8},{10,11... | collective-permute-start | bytes 196616 | tf_op jit(solution)/shard_map/ppermute | solution.py:283
  8.4 1.9 %collective-permute-start.1 = (bf16[4,32,256]{2,1,0:T(8,128)(2,1)S(1)}, bf16[4,32,256]{2,1,0:T(8,128)(2,1)S(1)}, u32[]{:S(2)}, u32[]{:S(2)}) collective-permute-start(bf16[4,32,256]{2,1,0:T(8,128)(2,1)S(1)} %get-tuple-element.25), channel_id=1, source_target_pairs={{1,2},{2,1},{5,6},{6,5},{9,10},{10,9},{13,14},{14,13},{17,18},{18,... | collective-permute-start | bytes 196616 | tf_op jit(solution)/shard_map/ppermute | solution.py:282
  10.4 1.9 %load.1 = (f32[16,9,8,128]{3,2,1,0:T(8,128)S(1)}, f32[16,9,8,128]{3,2,1,0:T(8,128)S(1)}, bf16[16,16,256]{2,1,0:T(8,128)(2,1)S(1)}, bf16[16,8,256]{2,1,0:T(8,128)...) custom-call(f32[64,64]{1,0:T(8,128)} %vert_hbm.1, ...), custom_call_target="tpu_custom_call" | custom-call | tf_op jit(solution)/shard_map/load/pallas_call | solution.py:286
  12.2 0.0 collective-permute-done.outer_ref
  12.3 2.3 %collective-permute-done.1.inner_ref = bf16[4,32,256]{2,1,0:T(8,128)(2,1)S(1)} collective-permute-done((bf16[4,32,256]{2,1,0:T(8,128)(2,1)S(1)}, bf16[4,32,256]{2,1,0:T(8,128)(2,1)S(1)}, u32[]{:S(2)}, u32[]{:S(2)}) %collective-permute-start.1) | collective-permute-done | bytes 65568 | tf_op jit(solution)/shard_map/ppermute | solution.py:282
  14.6 0.3 localize.1
  14.9 1.9 %collective-permute-start.2 = (bf16[144,128]{1,0:T(8,128)(2,1)S(1)}, bf16[144,128]{1,0:T(8,128)(2,1)S(1)}, u32[]{:S(2)}, u32[]{:S(2)}) collective-permute-start(bf16[144,128]{1,0:T(8,128)(2,1)S(1)} %get-tuple-element.28), channel_id=1, source_target_pairs={{0,4},{4,0},{8,12},{12,8},{16,20},{20,16},{24,28},{28,24},{32,36},... | collective-permute-start | bytes 110600 | tf_op jit(solution)/shard_map/ppermute | solution.py:315
  16.9 11.2 %collective-permute-start.3 = (bf16[144,128]{1,0:T(8,128)(2,1)S(1)}, bf16[144,128]{1,0:T(8,128)(2,1)S(1)}, u32[]{:S(2)}, u32[]{:S(2)}) collective-permute-start(bf16[144,128]{1,0:T(8,128)(2,1)S(1)} %get-tuple-element.29), channel_id=1, source_target_pairs={{0,508},{4,8},{8,4},{12,16},{16,12},{20,24},{24,20},{28,32},{32,28... | collective-permute-start | bytes 110600 | tf_op jit(solution)/shard_map/ppermute | solution.py:314
  28.0 1.2 %weights.1.matrix_ref = bf16[384,4096]{1,0:T(8,128)(2,1)S(1)} custom-call(s32[4,4096]{1,0:T(4,128)S(1)} %get-tuple-element.30.stencil_ref, bf16[4,4096]{1,0:T(4,128)(2,1)S(1)} %get-tuple-element.31.weight_ref), custom_call_target="tpu_custom_call" | custom-call | flops 25165824 | bytes 3145728 | tf_op jit(solution)/shard_map/weights/pallas_call | solution.py:295
  29.2 0.0 collective-permute-done.2.chip_ref
  29.2 1.0 %collective-permute-done.3.cross_ref = bf16[144,128]{1,0:T(8,128)(2,1)S(1)} collective-permute-done((bf16[144,128]{1,0:T(8,128)(2,1)S(1)}, bf16[144,128]{1,0:T(8,128)(2,1)S(1)}, u32[]{:S(2)}, u32[]{:S(2)}) %collective-permute-start.3) | collective-permute-done | bytes 36896 | tf_op jit(solution)/shard_map/ppermute | solution.py:314
  30.3 2.8 %fine.1 = (f32[272,256]{1,0:T(8,128)S(1)}, bf16[144,128]{1,0:T(8,128)(2,1)S(1)}, bf16[144,128]{1,0:T(8,128)(2,1)S(1)}) custom-call(bf16[272,256]{1,0:T(8,128)(2,1)S(1)} %get-tuple-element.27.own_ref, bf16[144,128]{1,0:T(8,128)(2,1)S(1)} %collective-permute-done.2.chip_ref, bf16[144,128]{1,0:T(8,128)(2,1)S(1)} %collective-permute-done.3.cross_ref, ...), custom_call_target="tpu_custom_call" | custom-call | tf_op jit(solution)/shard_map/fine/pallas_call | solution.py:316
  33.0 1.9 %collective-permute-start.4 = (bf16[144,128]{1,0:T(8,128)(2,1)S(1)}, bf16[144,128]{1,0:T(8,128)(2,1)S(1)}, u32[]{:S(2)}, u32[]{:S(2)}) collective-permute-start(bf16[144,128]{1,0:T(8,128)(2,1)S(1)} %get-tuple-element.34), channel_id=1, source_target_pairs={{0,4},{4,0},{8,12},{12,8},{16,20},{20,16},{24,28},{28,24},{32,36},... | collective-permute-start | bytes 110600 | tf_op jit(solution)/shard_map/ppermute | solution.py:325
  34.9 1.2 %collective-permute-done.4.chip_ref = bf16[144,128]{1,0:T(8,128)(2,1)S(1)} collective-permute-done((bf16[144,128]{1,0:T(8,128)(2,1)S(1)}, bf16[144,128]{1,0:T(8,128)(2,1)S(1)}, u32[]{:S(2)}, u32[]{:S(2)}) %collective-permute-start.4) | collective-permute-done | bytes 36896 | tf_op jit(solution)/shard_map/ppermute | solution.py:325
  36.1 0.1 merge.1
  36.2 17.8 %all_to_all.5.got_ref = bf16[8,144,128]{2,1,0:T(8,128)(2,1)S(1)} all-to-all(bf16[8,144,128]{2,1,0:T(8,128)(2,1)S(1)} %get-tuple-element.37), channel_id=1, replica_groups={{4,5,6,7,8,9,10,11},{12,13,14,15,16,17,18,19},{20,21,22,23,24,25,26,27}..., dimensions={0} | all-to-all | bytes 589824 | tf_op jit(solution)/shard_map/all_to_all | solution.py:336
  54.0 1.0 %finish.1 = (f32[16,16,256]{2,1,0:T(8,128)}, f32[16,8,256]{2,1,0:T(8,128)}) custom-call(f32[16,9,8,128]{3,2,1,0:T(8,128)S(1)} %get-tuple-element.20.band_ref, f32[272,256]{1,0:T(8,128)S(1)} %get-tuple-element.36.own_ref, bf16[8,144,128]{2,1,0:T(8,128)(2,1)S(1)} %all_to_all.5.got_ref, bf16[16,8,256]{2,1,0:T(8,128)(2,1)S(1)} %get-tuple-element.26.cp_ref, ...), custom_call_target="tpu_custom_call" | custom-call | tf_op jit(solution)/shard_map/finish/pallas_call | solution.py:338
Async XLA Ops:
  1.5 10.7 %collective-permute-start = (bf16[4,32,256]{2,1,0:T(8,128)(2,1)S(1)}, bf16[4,32,256]{2,1,0:T(8,128)(2,1)S(1)}, u32[]{:S(2)}, u32[]{:S(2)}) collective-permute-start(bf16[4,32,256]{2,1,0:T(8,128)(2,1)S(1)} %get-tuple-element.24), channel_id=1, source_target_pairs={{0,1},{1,0},{2,3},{3,2},{4,5},{5,4},{6,7},{7,6},{8,9},{9,8},{10,11... | collective-permute-start | bytes 196616 | tf_op jit(solution)/shard_map/ppermute | solution.py:283
  8.4 6.2 %collective-permute-start.1 = (bf16[4,32,256]{2,1,0:T(8,128)(2,1)S(1)}, bf16[4,32,256]{2,1,0:T(8,128)(2,1)S(1)}, u32[]{:S(2)}, u32[]{:S(2)}) collective-permute-start(bf16[4,32,256]{2,1,0:T(8,128)(2,1)S(1)} %get-tuple-element.25), channel_id=1, source_target_pairs={{1,2},{2,1},{5,6},{6,5},{9,10},{10,9},{13,14},{14,13},{17,18},{18,... | collective-permute-start | bytes 196616 | tf_op jit(solution)/shard_map/ppermute | solution.py:282
  14.9 14.3 %collective-permute-start.2 = (bf16[144,128]{1,0:T(8,128)(2,1)S(1)}, bf16[144,128]{1,0:T(8,128)(2,1)S(1)}, u32[]{:S(2)}, u32[]{:S(2)}) collective-permute-start(bf16[144,128]{1,0:T(8,128)(2,1)S(1)} %get-tuple-element.28), channel_id=1, source_target_pairs={{0,4},{4,0},{8,12},{12,8},{16,20},{20,16},{24,28},{28,24},{32,36},... | collective-permute-start | bytes 110600 | tf_op jit(solution)/shard_map/ppermute | solution.py:315
  16.9 13.4 %collective-permute-start.3 = (bf16[144,128]{1,0:T(8,128)(2,1)S(1)}, bf16[144,128]{1,0:T(8,128)(2,1)S(1)}, u32[]{:S(2)}, u32[]{:S(2)}) collective-permute-start(bf16[144,128]{1,0:T(8,128)(2,1)S(1)} %get-tuple-element.29), channel_id=1, source_target_pairs={{0,508},{4,8},{8,4},{12,16},{16,12},{20,24},{24,20},{28,32},{32,28... | collective-permute-start | bytes 110600 | tf_op jit(solution)/shard_map/ppermute | solution.py:314
  33.0 3.1 %collective-permute-start.4 = (bf16[144,128]{1,0:T(8,128)(2,1)S(1)}, bf16[144,128]{1,0:T(8,128)(2,1)S(1)}, u32[]{:S(2)}, u32[]{:S(2)}) collective-permute-start(bf16[144,128]{1,0:T(8,128)(2,1)S(1)} %get-tuple-element.34), channel_id=1, source_target_pairs={{0,4},{4,0},{8,12},{12,8},{16,20},{20,16},{24,28},{28,24},{32,36},... | collective-permute-start | bytes 110600 | tf_op jit(solution)/shard_map/ppermute | solution.py:325

commit v3 on v2

--- a/solution.py
+++ b/solution.py
@@ -15,6 +15,7 @@
 NF = 4096
 WL = LV + 2 * HB
 LEVS = 4
+LEAD = 1
 BAND = 2 * HB + 1
 ROWS = LV * MB + LV
 HALF = 144
@@ -32,6 +33,10 @@
 
 def odd_tile():
     return lax.axis_index("tile") % 2
+
+
+def slot(lev):
+    return (lev + LEVS - LEAD) % LEVS
 
 
 def odd_lev():
@@ -191,7 +196,7 @@
         rows = slice(first * MB, first * MB + edge)
         row = slice(LV * MB + first, LV * MB + first + HB)
         parts = [own_out[rows, : 2 * CW], own_out[rows, 2 * CW :], own_out[row, : 2 * CW], own_out[row, 2 * CW :], blank]
-        send_ref[here + place] = jnp.concatenate(parts, axis=0).astype(BF16)
+        send_ref[here + slot(place)] = jnp.concatenate(parts, axis=0).astype(BF16)
 
 
 def finish_kernel(band_ref, own_ref, got_ref, cp_ref, outer_ref, inner_ref, member_hbm, coarse_hbm, ms, cs, member_out, coarse_out, sems):
@@ -204,7 +209,7 @@
     upper = jnp.minimum(lev + 1, LEVS - 1)
     wide = 2 * CW
     edge = HB * MB
-    lead, trail = joined(got_ref[there + lev], odd)
+    lead, trail = joined(got_ref[there + slot(lev)], odd)
     for i in range(LV):
         rows = slice(i * MB, (i + 1) * MB)
         row = slice(LV * MB + i, LV * MB + i + 1)
@@ -214,8 +219,8 @@
         cs[HB + i, :, :wide] = pert[:, :wide] * (own_ref[row, :wide] + lead[row])
         cs[HB + i, :, wide:] = pert[:, wide:] * (own_ref[row, wide:] + trail[row])
     for place, first, base, below in ((lower, LV - HB, 0, swapped), (upper, 0, HB + LV, ~swapped)):
-        lead, trail = joined(got_ref[there + place], odd)
-        near = got_ref[here + place].astype(F32)
+        lead, trail = joined(got_ref[there + slot(place)], odd)
+        near = got_ref[here + slot(place)].astype(F32)
         near = jnp.where(place == lev, 0.0, near)
         lead = jnp.where(place == lev, 0.0, lead)
         trail = jnp.where(place == lev, 0.0, trail)
@@ -332,7 +337,7 @@
         name="merge",
     )(*near(own, chip, cross))
     pairs = [(t, (t + 1) % tiles) if t + 1 != tiles // 2 else (t + 1, t) for t in range(1, tiles, 2)]
-    groups = [[t * levs + z for t in pair for z in range(levs)] for pair in pairs]
+    groups = [[t * levs + (z + LEAD) % levs for t in pair for z in range(levs)] for pair in pairs]
     got = lax.all_to_all(send, ("tile", "lev"), 0, 0, axis_index_groups=groups)
     finals = (shape((LV, MB, ND), F32), shape((LV, CM, ND), F32))
     return pl.pallas_call(

time: 55.4 us -> 53.8 us (0.971)
  blocking collectives: 17.8 us -> 16.2 us
    all_to_all x1, blocking collectives: 17.8 us -> 16.2 us  [shards(): got = lax.all_to_all(send, ('tile', 'lev'), 0, 0, axis_index_groups=groups)]
where the time goes in v3:
time: 53.8 us; the launch traced here: 53.4 us
  starting transfers between devices  23.8 us (44%)
  blocking collectives  16.2 us (30%)
  Pallas kernels  8.15 us (15%)
  waiting for transfers between devices  4.57 us (8%)
  between operations  0.72 us (1%)
    all_to_all x1, blocking collectives, shards(): got = lax.all_to_all(send, ('tile', 'lev'), 0, 0, axis_index_groups=groups)  16.2 us
    ppermute x1, starting transfers between devices, shards(): cross = lax.ppermute(cross, 'tile', off_chip)  11.2 us
    ppermute x1, starting transfers between devices, shards(): outer = lax.ppermute(outer, 'lev', outer_pairs)  6.91 us
    ppermute x2, starting transfers between devices, shards(): chip = lax.ppermute(chip, 'tile', on_chip)  3.84 us
    pallas_call x1, Pallas kernels, shards(): pl.pallas_call(fine_kernel, out_shape=(pltpu.VMEM((ROWS, ND), F32), packe...  2.75 us
    ppermute x1, waiting for transfers between devices, shards(): inner = lax.ppermute(inner, 'lev', inner_pairs)  2.34 us
    ppermute x1, starting transfers between devices, shards(): inner = lax.ppermute(inner, 'lev', inner_pairs)  1.92 us
    pallas_call x1, Pallas kernels, shards(): pl.pallas_call(load_kernel, out_shape=(splats, splats, *[pltpu.VMEM(x.sha...  1.88 us
  transfers between devices with their start and end apart: 5, of which 3 were waited for; matrix products, arithmetic and copies ran while one was open for 0% of the time, Pallas kernels for 6%

profile of v3, /device:TPU:64, one launch (start us, length us, event | category | flops | bytes accessed | tf_op | source)
XLA Modules:
  0.0 53.4 jit_solution(17148642246130667613)
XLA Ops:
  0.6 0.9 %edges.1 = (bf16[4,32,256]{2,1,0:T(8,128)(2,1)S(1)}, bf16[4,32,256]{2,1,0:T(8,128)(2,1)S(1)}) custom-call(bf16[16,16,256]{2,1,0:T(8,128)(2,1)} %mc_hbm.3, bf16[16,8,256]{2,1,0:T(8,128)(2,1)} %cc_hbm.3, bf16[16,8,256]{2,1,0:T(8,128)(2,1)} %cp_hbm.3), custom_call_target="tpu_custom_call" | custom-call | tf_op jit(solution)/shard_map/edges/pallas_call | solution.py:278
  1.5 6.9 %collective-permute-start = (bf16[4,32,256]{2,1,0:T(8,128)(2,1)S(1)}, bf16[4,32,256]{2,1,0:T(8,128)(2,1)S(1)}, u32[]{:S(2)}, u32[]{:S(2)}) collective-permute-start(bf16[4,32,256]{2,1,0:T(8,128)(2,1)S(1)} %get-tuple-element.24), channel_id=1, source_target_pairs={{0,1},{1,0},{2,3},{3,2},{4,5},{5,4},{6,7},{7,6},{8,9},{9,8},{10,11... | collective-permute-start | bytes 196616 | tf_op jit(solution)/shard_map/ppermute | solution.py:288
  8.4 1.9 %collective-permute-start.1 = (bf16[4,32,256]{2,1,0:T(8,128)(2,1)S(1)}, bf16[4,32,256]{2,1,0:T(8,128)(2,1)S(1)}, u32[]{:S(2)}, u32[]{:S(2)}) collective-permute-start(bf16[4,32,256]{2,1,0:T(8,128)(2,1)S(1)} %get-tuple-element.25), channel_id=1, source_target_pairs={{1,2},{2,1},{5,6},{6,5},{9,10},{10,9},{13,14},{14,13},{17,18},{18,... | collective-permute-start | bytes 196616 | tf_op jit(solution)/shard_map/ppermute | solution.py:287
  10.4 1.9 %load.1 = (f32[16,9,8,128]{3,2,1,0:T(8,128)S(1)}, f32[16,9,8,128]{3,2,1,0:T(8,128)S(1)}, bf16[16,16,256]{2,1,0:T(8,128)(2,1)S(1)}, bf16[16,8,256]{2,1,0:T(8,128)...) custom-call(f32[64,64]{1,0:T(8,128)} %vert_hbm.1, ...), custom_call_target="tpu_custom_call" | custom-call | tf_op jit(solution)/shard_map/load/pallas_call | solution.py:291
  12.2 0.0 collective-permute-done.outer_ref
  12.3 2.3 %collective-permute-done.1.inner_ref = bf16[4,32,256]{2,1,0:T(8,128)(2,1)S(1)} collective-permute-done((bf16[4,32,256]{2,1,0:T(8,128)(2,1)S(1)}, bf16[4,32,256]{2,1,0:T(8,128)(2,1)S(1)}, u32[]{:S(2)}, u32[]{:S(2)}) %collective-permute-start.1) | collective-permute-done | bytes 65568 | tf_op jit(solution)/shard_map/ppermute | solution.py:287
  14.6 0.3 localize.1
  14.9 1.9 %collective-permute-start.2 = (bf16[144,128]{1,0:T(8,128)(2,1)S(1)}, bf16[144,128]{1,0:T(8,128)(2,1)S(1)}, u32[]{:S(2)}, u32[]{:S(2)}) collective-permute-start(bf16[144,128]{1,0:T(8,128)(2,1)S(1)} %get-tuple-element.28), channel_id=1, source_target_pairs={{0,4},{4,0},{8,12},{12,8},{16,20},{20,16},{24,28},{28,24},{32,36},... | collective-permute-start | bytes 110600 | tf_op jit(solution)/shard_map/ppermute | solution.py:320
  16.9 11.2 %collective-permute-start.3 = (bf16[144,128]{1,0:T(8,128)(2,1)S(1)}, bf16[144,128]{1,0:T(8,128)(2,1)S(1)}, u32[]{:S(2)}, u32[]{:S(2)}) collective-permute-start(bf16[144,128]{1,0:T(8,128)(2,1)S(1)} %get-tuple-element.29), channel_id=1, source_target_pairs={{0,508},{4,8},{8,4},{12,16},{16,12},{20,24},{24,20},{28,32},{32,28... | collective-permute-start | bytes 110600 | tf_op jit(solution)/shard_map/ppermute | solution.py:319
  28.0 1.2 %weights.1.matrix_ref = bf16[384,4096]{1,0:T(8,128)(2,1)S(1)} custom-call(s32[4,4096]{1,0:T(4,128)S(1)} %get-tuple-element.30.stencil_ref, bf16[4,4096]{1,0:T(4,128)(2,1)S(1)} %get-tuple-element.31.weight_ref), custom_call_target="tpu_custom_call" | custom-call | flops 25165824 | bytes 3145728 | tf_op jit(solution)/shard_map/weights/pallas_call | solution.py:300
  29.2 0.0 collective-permute-done.2.chip_ref
  29.2 1.0 %collective-permute-done.3.cross_ref = bf16[144,128]{1,0:T(8,128)(2,1)S(1)} collective-permute-done((bf16[144,128]{1,0:T(8,128)(2,1)S(1)}, bf16[144,128]{1,0:T(8,128)(2,1)S(1)}, u32[]{:S(2)}, u32[]{:S(2)}) %collective-permute-start.3) | collective-permute-done | bytes 36896 | tf_op jit(solution)/shard_map/ppermute | solution.py:319
  30.3 2.8 %fine.1 = (f32[272,256]{1,0:T(8,128)S(1)}, bf16[144,128]{1,0:T(8,128)(2,1)S(1)}, bf16[144,128]{1,0:T(8,128)(2,1)S(1)}) custom-call(bf16[272,256]{1,0:T(8,128)(2,1)S(1)} %get-tuple-element.27.own_ref, bf16[144,128]{1,0:T(8,128)(2,1)S(1)} %collective-permute-done.2.chip_ref, bf16[144,128]{1,0:T(8,128)(2,1)S(1)} %collective-permute-done.3.cross_ref, ...), custom_call_target="tpu_custom_call" | custom-call | tf_op jit(solution)/shard_map/fine/pallas_call | solution.py:321
  33.0 1.9 %collective-permute-start.4 = (bf16[144,128]{1,0:T(8,128)(2,1)S(1)}, bf16[144,128]{1,0:T(8,128)(2,1)S(1)}, u32[]{:S(2)}, u32[]{:S(2)}) collective-permute-start(bf16[144,128]{1,0:T(8,128)(2,1)S(1)} %get-tuple-element.34), channel_id=1, source_target_pairs={{0,4},{4,0},{8,12},{12,8},{16,20},{20,16},{24,28},{28,24},{32,36},... | collective-permute-start | bytes 110600 | tf_op jit(solution)/shard_map/ppermute | solution.py:330
  34.9 1.2 %collective-permute-done.4.chip_ref = bf16[144,128]{1,0:T(8,128)(2,1)S(1)} collective-permute-done((bf16[144,128]{1,0:T(8,128)(2,1)S(1)}, bf16[144,128]{1,0:T(8,128)(2,1)S(1)}, u32[]{:S(2)}, u32[]{:S(2)}) %collective-permute-start.4) | collective-permute-done | bytes 36896 | tf_op jit(solution)/shard_map/ppermute | solution.py:330
  36.1 0.1 merge.1
  36.2 16.2 %all_to_all.5.got_ref = bf16[8,144,128]{2,1,0:T(8,128)(2,1)S(1)} all-to-all(bf16[8,144,128]{2,1,0:T(8,128)(2,1)S(1)} %get-tuple-element.37), channel_id=1, replica_groups={{5,6,7,4,9,10,11,8},{13,14,15,12,17,18,19,16},{21,22,23,20,25,26,27,24}..., dimensions={0} | all-to-all | bytes 589824 | tf_op jit(solution)/shard_map/all_to_all | solution.py:341
  52.4 1.0 %finish.1 = (f32[16,16,256]{2,1,0:T(8,128)}, f32[16,8,256]{2,1,0:T(8,128)}) custom-call(f32[16,9,8,128]{3,2,1,0:T(8,128)S(1)} %get-tuple-element.20.band_ref, f32[272,256]{1,0:T(8,128)S(1)} %get-tuple-element.36.own_ref, bf16[8,144,128]{2,1,0:T(8,128)(2,1)S(1)} %all_to_all.5.got_ref, bf16[16,8,256]{2,1,0:T(8,128)(2,1)S(1)} %get-tuple-element.26.cp_ref, ...), custom_call_target="tpu_custom_call" | custom-call | tf_op jit(solution)/shard_map/finish/pallas_call | solution.py:343
Async XLA Ops:
  1.5 10.7 %collective-permute-start = (bf16[4,32,256]{2,1,0:T(8,128)(2,1)S(1)}, bf16[4,32,256]{2,1,0:T(8,128)(2,1)S(1)}, u32[]{:S(2)}, u32[]{:S(2)}) collective-permute-start(bf16[4,32,256]{2,1,0:T(8,128)(2,1)S(1)} %get-tuple-element.24), channel_id=1, source_target_pairs={{0,1},{1,0},{2,3},{3,2},{4,5},{5,4},{6,7},{7,6},{8,9},{9,8},{10,11... | collective-permute-start | bytes 196616 | tf_op jit(solution)/shard_map/ppermute | solution.py:288
  8.4 6.2 %collective-permute-start.1 = (bf16[4,32,256]{2,1,0:T(8,128)(2,1)S(1)}, bf16[4,32,256]{2,1,0:T(8,128)(2,1)S(1)}, u32[]{:S(2)}, u32[]{:S(2)}) collective-permute-start(bf16[4,32,256]{2,1,0:T(8,128)(2,1)S(1)} %get-tuple-element.25), channel_id=1, source_target_pairs={{1,2},{2,1},{5,6},{6,5},{9,10},{10,9},{13,14},{14,13},{17,18},{18,... | collective-permute-start | bytes 196616 | tf_op jit(solution)/shard_map/ppermute | solution.py:287
  14.9 14.3 %collective-permute-start.2 = (bf16[144,128]{1,0:T(8,128)(2,1)S(1)}, bf16[144,128]{1,0:T(8,128)(2,1)S(1)}, u32[]{:S(2)}, u32[]{:S(2)}) collective-permute-start(bf16[144,128]{1,0:T(8,128)(2,1)S(1)} %get-tuple-element.28), channel_id=1, source_target_pairs={{0,4},{4,0},{8,12},{12,8},{16,20},{20,16},{24,28},{28,24},{32,36},... | collective-permute-start | bytes 110600 | tf_op jit(solution)/shard_map/ppermute | solution.py:320
  16.9 13.4 %collective-permute-start.3 = (bf16[144,128]{1,0:T(8,128)(2,1)S(1)}, bf16[144,128]{1,0:T(8,128)(2,1)S(1)}, u32[]{:S(2)}, u32[]{:S(2)}) collective-permute-start(bf16[144,128]{1,0:T(8,128)(2,1)S(1)} %get-tuple-element.29), channel_id=1, source_target_pairs={{0,508},{4,8},{8,4},{12,16},{16,12},{20,24},{24,20},{28,32},{32,28... | collective-permute-start | bytes 110600 | tf_op jit(solution)/shard_map/ppermute | solution.py:319
  33.0 3.1 %collective-permute-start.4 = (bf16[144,128]{1,0:T(8,128)(2,1)S(1)}, bf16[144,128]{1,0:T(8,128)(2,1)S(1)}, u32[]{:S(2)}, u32[]{:S(2)}) collective-permute-start(bf16[144,128]{1,0:T(8,128)(2,1)S(1)} %get-tuple-element.34), channel_id=1, source_target_pairs={{0,4},{4,0},{8,12},{12,8},{16,20},{20,16},{24,28},{28,24},{32,36},... | collective-permute-start | bytes 110600 | tf_op jit(solution)/shard_map/ppermute | solution.py:330

commit v4 on v3

--- a/solution.py
+++ b/solution.py
@@ -22,6 +22,7 @@
 SPAN = ND + 2 * CW
 BLOCK = 512
 STEP = 2048
+OUT = 2
 F32 = jnp.float32
 BF16 = jnp.bfloat16
 VMEM = pl.BlockSpec(memory_space=pltpu.VMEM)
@@ -242,8 +243,8 @@
             coarse = coarse + scaled(band_ref[j, d], cs[j + d])
         member_out[j] = member
         coarse_out[j] = coarse
-        if j % HB == HB - 1:
-            span = pl.ds(j + 1 - HB, HB)
+        if j % OUT == OUT - 1:
+            span = pl.ds(j + 1 - OUT, OUT)
             for source, target in ((member_out, member_hbm), (coarse_out, coarse_hbm)):
                 copies.append(pltpu.make_async_copy(source.at[span], target.at[span], sems.at[len(copies)]))
                 copies[-1].start()
@@ -350,7 +351,7 @@
             pltpu.VMEM((WL, CM, ND), F32),
             pltpu.VMEM((LV, MB, ND), F32),
             pltpu.VMEM((LV, CM, ND), F32),
-            pltpu.SemaphoreType.DMA((2 * LV // HB,)),
+            pltpu.SemaphoreType.DMA((2 * LV // OUT,)),
         ],
         compiler_params=PARAMS,
         name="finish",

time: 53.8 us -> 54 us (level)
  no operation moved by 1% of the time
where the time goes in v4:
time: 54 us; the launch traced here: 53.6 us
  starting transfers between devices  23.8 us (44%)
  blocking collectives  16.2 us (30%)
  Pallas kernels  8.31 us (15%)
  waiting for transfers between devices  4.57 us (8%)
  between operations  0.72 us (1%)
    all_to_all x1, blocking collectives, shards(): got = lax.all_to_all(send, ('tile', 'lev'), 0, 0, axis_index_groups=groups)  16.2 us
    ppermute x1, starting transfers between devices, shards(): cross = lax.ppermute(cross, 'tile', off_chip)  11.2 us
    ppermute x1, starting transfers between devices, shards(): outer = lax.ppermute(outer, 'lev', outer_pairs)  6.91 us
    ppermute x2, starting transfers between devices, shards(): chip = lax.ppermute(chip, 'tile', on_chip)  3.84 us
    pallas_call x1, Pallas kernels, shards(): pl.pallas_call(fine_kernel, out_shape=(pltpu.VMEM((ROWS, ND), F32), packe...  2.75 us
    ppermute x1, waiting for transfers between devices, shards(): inner = lax.ppermute(inner, 'lev', inner_pairs)  2.34 us
    ppermute x1, starting transfers between devices, shards(): inner = lax.ppermute(inner, 'lev', inner_pairs)  1.92 us
    pallas_call x1, Pallas kernels, shards(): pl.pallas_call(load_kernel, out_shape=(splats, splats, *[pltpu.VMEM(x.sha...  1.88 us
  transfers between devices with their start and end apart: 5, of which 3 were waited for; matrix products, arithmetic and copies ran while one was open for 0% of the time, Pallas kernels for 6%

profile of v4, /device:TPU:64, one launch (start us, length us, event | category | flops | bytes accessed | tf_op | source)
XLA Modules:
  0.0 53.6 jit_solution(14735294077200337537)
XLA Ops:
  0.6 0.9 %edges.1 = (bf16[4,32,256]{2,1,0:T(8,128)(2,1)S(1)}, bf16[4,32,256]{2,1,0:T(8,128)(2,1)S(1)}) custom-call(bf16[16,16,256]{2,1,0:T(8,128)(2,1)} %mc_hbm.3, bf16[16,8,256]{2,1,0:T(8,128)(2,1)} %cc_hbm.3, bf16[16,8,256]{2,1,0:T(8,128)(2,1)} %cp_hbm.3), custom_call_target="tpu_custom_call" | custom-call | tf_op jit(solution)/shard_map/edges/pallas_call | solution.py:279
  1.5 6.9 %collective-permute-start = (bf16[4,32,256]{2,1,0:T(8,128)(2,1)S(1)}, bf16[4,32,256]{2,1,0:T(8,128)(2,1)S(1)}, u32[]{:S(2)}, u32[]{:S(2)}) collective-permute-start(bf16[4,32,256]{2,1,0:T(8,128)(2,1)S(1)} %get-tuple-element.24), channel_id=1, source_target_pairs={{0,1},{1,0},{2,3},{3,2},{4,5},{5,4},{6,7},{7,6},{8,9},{9,8},{10,11... | collective-permute-start | bytes 196616 | tf_op jit(solution)/shard_map/ppermute | solution.py:289
  8.4 1.9 %collective-permute-start.1 = (bf16[4,32,256]{2,1,0:T(8,128)(2,1)S(1)}, bf16[4,32,256]{2,1,0:T(8,128)(2,1)S(1)}, u32[]{:S(2)}, u32[]{:S(2)}) collective-permute-start(bf16[4,32,256]{2,1,0:T(8,128)(2,1)S(1)} %get-tuple-element.25), channel_id=1, source_target_pairs={{1,2},{2,1},{5,6},{6,5},{9,10},{10,9},{13,14},{14,13},{17,18},{18,... | collective-permute-start | bytes 196616 | tf_op jit(solution)/shard_map/ppermute | solution.py:288
  10.4 1.9 %load.1 = (f32[16,9,8,128]{3,2,1,0:T(8,128)S(1)}, f32[16,9,8,128]{3,2,1,0:T(8,128)S(1)}, bf16[16,16,256]{2,1,0:T(8,128)(2,1)S(1)}, bf16[16,8,256]{2,1,0:T(8,128)...) custom-call(f32[64,64]{1,0:T(8,128)} %vert_hbm.1, ...), custom_call_target="tpu_custom_call" | custom-call | tf_op jit(solution)/shard_map/load/pallas_call | solution.py:292
  12.2 0.0 collective-permute-done.outer_ref
  12.3 2.3 %collective-permute-done.1.inner_ref = bf16[4,32,256]{2,1,0:T(8,128)(2,1)S(1)} collective-permute-done((bf16[4,32,256]{2,1,0:T(8,128)(2,1)S(1)}, bf16[4,32,256]{2,1,0:T(8,128)(2,1)S(1)}, u32[]{:S(2)}, u32[]{:S(2)}) %collective-permute-start.1) | collective-permute-done | bytes 65568 | tf_op jit(solution)/shard_map/ppermute | solution.py:288
  14.6 0.3 localize.1
  14.9 1.9 %collective-permute-start.2 = (bf16[144,128]{1,0:T(8,128)(2,1)S(1)}, bf16[144,128]{1,0:T(8,128)(2,1)S(1)}, u32[]{:S(2)}, u32[]{:S(2)}) collective-permute-start(bf16[144,128]{1,0:T(8,128)(2,1)S(1)} %get-tuple-element.28), channel_id=1, source_target_pairs={{0,4},{4,0},{8,12},{12,8},{16,20},{20,16},{24,28},{28,24},{32,36},... | collective-permute-start | bytes 110600 | tf_op jit(solution)/shard_map/ppermute | solution.py:321
  16.9 11.2 %collective-permute-start.3 = (bf16[144,128]{1,0:T(8,128)(2,1)S(1)}, bf16[144,128]{1,0:T(8,128)(2,1)S(1)}, u32[]{:S(2)}, u32[]{:S(2)}) collective-permute-start(bf16[144,128]{1,0:T(8,128)(2,1)S(1)} %get-tuple-element.29), channel_id=1, source_target_pairs={{0,508},{4,8},{8,4},{12,16},{16,12},{20,24},{24,20},{28,32},{32,28... | collective-permute-start | bytes 110600 | tf_op jit(solution)/shard_map/ppermute | solution.py:320
  28.0 1.2 %weights.1.matrix_ref = bf16[384,4096]{1,0:T(8,128)(2,1)S(1)} custom-call(s32[4,4096]{1,0:T(4,128)S(1)} %get-tuple-element.30.stencil_ref, bf16[4,4096]{1,0:T(4,128)(2,1)S(1)} %get-tuple-element.31.weight_ref), custom_call_target="tpu_custom_call" | custom-call | flops 25165824 | bytes 3145728 | tf_op jit(solution)/shard_map/weights/pallas_call | solution.py:301
  29.2 0.0 collective-permute-done.2.chip_ref
  29.2 1.0 %collective-permute-done.3.cross_ref = bf16[144,128]{1,0:T(8,128)(2,1)S(1)} collective-permute-done((bf16[144,128]{1,0:T(8,128)(2,1)S(1)}, bf16[144,128]{1,0:T(8,128)(2,1)S(1)}, u32[]{:S(2)}, u32[]{:S(2)}) %collective-permute-start.3) | collective-permute-done | bytes 36896 | tf_op jit(solution)/shard_map/ppermute | solution.py:320
  30.3 2.8 %fine.1 = (f32[272,256]{1,0:T(8,128)S(1)}, bf16[144,128]{1,0:T(8,128)(2,1)S(1)}, bf16[144,128]{1,0:T(8,128)(2,1)S(1)}) custom-call(bf16[272,256]{1,0:T(8,128)(2,1)S(1)} %get-tuple-element.27.own_ref, bf16[144,128]{1,0:T(8,128)(2,1)S(1)} %collective-permute-done.2.chip_ref, bf16[144,128]{1,0:T(8,128)(2,1)S(1)} %collective-permute-done.3.cross_ref, ...), custom_call_target="tpu_custom_call" | custom-call | tf_op jit(solution)/shard_map/fine/pallas_call | solution.py:322
  33.0 1.9 %collective-permute-start.4 = (bf16[144,128]{1,0:T(8,128)(2,1)S(1)}, bf16[144,128]{1,0:T(8,128)(2,1)S(1)}, u32[]{:S(2)}, u32[]{:S(2)}) collective-permute-start(bf16[144,128]{1,0:T(8,128)(2,1)S(1)} %get-tuple-element.34), channel_id=1, source_target_pairs={{0,4},{4,0},{8,12},{12,8},{16,20},{20,16},{24,28},{28,24},{32,36},... | collective-permute-start | bytes 110600 | tf_op jit(solution)/shard_map/ppermute | solution.py:331
  34.9 1.2 %collective-permute-done.4.chip_ref = bf16[144,128]{1,0:T(8,128)(2,1)S(1)} collective-permute-done((bf16[144,128]{1,0:T(8,128)(2,1)S(1)}, bf16[144,128]{1,0:T(8,128)(2,1)S(1)}, u32[]{:S(2)}, u32[]{:S(2)}) %collective-permute-start.4) | collective-permute-done | bytes 36896 | tf_op jit(solution)/shard_map/ppermute | solution.py:331
  36.1 0.1 merge.1
  36.2 16.2 %all_to_all.5.got_ref = bf16[8,144,128]{2,1,0:T(8,128)(2,1)S(1)} all-to-all(bf16[8,144,128]{2,1,0:T(8,128)(2,1)S(1)} %get-tuple-element.37), channel_id=1, replica_groups={{5,6,7,4,9,10,11,8},{13,14,15,12,17,18,19,16},{21,22,23,20,25,26,27,24}..., dimensions={0} | all-to-all | bytes 589824 | tf_op jit(solution)/shard_map/all_to_all | solution.py:342
  52.4 1.2 %finish.1 = (f32[16,16,256]{2,1,0:T(8,128)}, f32[16,8,256]{2,1,0:T(8,128)}) custom-call(f32[16,9,8,128]{3,2,1,0:T(8,128)S(1)} %get-tuple-element.20.band_ref, f32[272,256]{1,0:T(8,128)S(1)} %get-tuple-element.36.own_ref, bf16[8,144,128]{2,1,0:T(8,128)(2,1)S(1)} %all_to_all.5.got_ref, bf16[16,8,256]{2,1,0:T(8,128)(2,1)S(1)} %get-tuple-element.26.cp_ref, ...), custom_call_target="tpu_custom_call" | custom-call | tf_op jit(solution)/shard_map/finish/pallas_call | solution.py:344
Async XLA Ops:
  1.5 10.7 %collective-permute-start = (bf16[4,32,256]{2,1,0:T(8,128)(2,1)S(1)}, bf16[4,32,256]{2,1,0:T(8,128)(2,1)S(1)}, u32[]{:S(2)}, u32[]{:S(2)}) collective-permute-start(bf16[4,32,256]{2,1,0:T(8,128)(2,1)S(1)} %get-tuple-element.24), channel_id=1, source_target_pairs={{0,1},{1,0},{2,3},{3,2},{4,5},{5,4},{6,7},{7,6},{8,9},{9,8},{10,11... | collective-permute-start | bytes 196616 | tf_op jit(solution)/shard_map/ppermute | solution.py:289
  8.4 6.2 %collective-permute-start.1 = (bf16[4,32,256]{2,1,0:T(8,128)(2,1)S(1)}, bf16[4,32,256]{2,1,0:T(8,128)(2,1)S(1)}, u32[]{:S(2)}, u32[]{:S(2)}) collective-permute-start(bf16[4,32,256]{2,1,0:T(8,128)(2,1)S(1)} %get-tuple-element.25), channel_id=1, source_target_pairs={{1,2},{2,1},{5,6},{6,5},{9,10},{10,9},{13,14},{14,13},{17,18},{18,... | collective-permute-start | bytes 196616 | tf_op jit(solution)/shard_map/ppermute | solution.py:288
  14.9 14.3 %collective-permute-start.2 = (bf16[144,128]{1,0:T(8,128)(2,1)S(1)}, bf16[144,128]{1,0:T(8,128)(2,1)S(1)}, u32[]{:S(2)}, u32[]{:S(2)}) collective-permute-start(bf16[144,128]{1,0:T(8,128)(2,1)S(1)} %get-tuple-element.28), channel_id=1, source_target_pairs={{0,4},{4,0},{8,12},{12,8},{16,20},{20,16},{24,28},{28,24},{32,36},... | collective-permute-start | bytes 110600 | tf_op jit(solution)/shard_map/ppermute | solution.py:321
  16.9 13.4 %collective-permute-start.3 = (bf16[144,128]{1,0:T(8,128)(2,1)S(1)}, bf16[144,128]{1,0:T(8,128)(2,1)S(1)}, u32[]{:S(2)}, u32[]{:S(2)}) collective-permute-start(bf16[144,128]{1,0:T(8,128)(2,1)S(1)} %get-tuple-element.29), channel_id=1, source_target_pairs={{0,508},{4,8},{8,4},{12,16},{16,12},{20,24},{24,20},{28,32},{32,28... | collective-permute-start | bytes 110600 | tf_op jit(solution)/shard_map/ppermute | solution.py:320
  33.0 3.1 %collective-permute-start.4 = (bf16[144,128]{1,0:T(8,128)(2,1)S(1)}, bf16[144,128]{1,0:T(8,128)(2,1)S(1)}, u32[]{:S(2)}, u32[]{:S(2)}) collective-permute-start(bf16[144,128]{1,0:T(8,128)(2,1)S(1)} %get-tuple-element.34), channel_id=1, source_target_pairs={{0,4},{4,0},{8,12},{12,8},{16,20},{20,16},{24,28},{28,24},{32,36},... | collective-permute-start | bytes 110600 | tf_op jit(solution)/shard_map/ppermute | solution.py:331
